TPU v7x, 256 devices: a whole 4x4x8 slice. The times are simulated.
256 devices in a mesh: seq: 32 (over x, z), head: 8 (over y, core).
Axes of the slice: x: 4, y: 4, z: 8, core: 2. Of those that a mesh axis runs over, the one named last changes fastest.
Arguments:
- queries: bfloat16 [32768, 4096], P('seq', 'head'), may hold values from -100 to 100
- keys: bfloat16 [32768, 4096], P('seq', 'head'), may hold values from -8 to 8
- values: bfloat16 [32768, 4096], P('seq', 'head'), may hold values from -6 to 6
- rates: float32 [32768, 16], P('seq', 'head'), may hold values from 0.001 to 0.01
- head_scale: float32 [16], P('head'), may hold values from 0.3 to 3
- w_one: float32 [16, 256, 256], P('head'), may hold values from -0.375 to 0.375
- w_three: float32 [16, 256, 256], P('head'), may hold values from -0.375 to 0.375
- w_two: float32 [16, 256, 256], P('head'), may hold values from -0.375 to 0.375
Outputs:
- mixed: float32 [32768, 4096], P('seq', 'head')
- new_one: float32 [16, 256, 256], P('head')
- new_three: float32 [16, 256, 256], P('head')
- new_two: float32 [16, 256, 256], P('head')
All inputs are finite; a program needn't handle non-finite values.
Results may differ from a plain program's by a relative error of at most 0.00065.
Values may be sent and summed in bfloat16 or wider, within the bound.
A program may use at most 64 MiB of HBM per device.

v0:
```python
import jax
import jax.numpy as jnp
from jax import lax
from jax.sharding import PartitionSpec as P

WINDOW_SPAN = 512


HIGH = lax.Precision.HIGHEST
EPS = 1e-06


def cut_along(value, dim, peers):
    shape = value.shape
    pieces = value.reshape(*shape[:dim], peers, shape[dim] // peers, *shape[dim + 1 :])
    return jnp.moveaxis(pieces, dim, 0)


def sum_at_owner(value, axis, dim):
    pieces = cut_along(value, dim, lax.axis_size(axis))
    arrived = lax.all_to_all(pieces, axis, split_axis=0, concat_axis=0, tiled=True)
    return arrived.sum(axis=0)


def joined_along(pieces, dim):
    pieces = jnp.moveaxis(pieces, 0, dim)
    shape = pieces.shape
    return pieces.reshape(*shape[:dim], shape[dim] * shape[dim + 1], *shape[dim + 2 :])


def from_everyone(value, axis):
    copies = jnp.broadcast_to(value, (lax.axis_size(axis), *value.shape))
    return lax.all_to_all(copies, axis, split_axis=0, concat_axis=0, tiled=True)


def collect(value, axis, dim):
    return joined_along(from_everyone(value, axis), dim)


def of_everyone(value, axis):
    everything = from_everyone(value, axis)
    return jnp.sum(everything, axis=0)


def passed_along(block, axis, distance):
    devices = range(lax.axis_size(axis))
    route = [(i - distance, i) for i in devices if i - distance in devices]
    return lax.ppermute(block, axis, route)


def renorm(weight, grad):
    upd = weight + grad
    old = jnp.sqrt(jnp.sum(weight * weight, axis=2, keepdims=True) + EPS)
    cur = jnp.sqrt(jnp.sum(upd * upd, axis=2, keepdims=True) + EPS)
    return upd * (old / cur)


def per_device(queries, keys, values, rates, head_scale, w_one, w_three, w_two):
    tokens, width = queries.shape
    head_group = w_one.shape[0]
    span_size = w_one.shape[1]
    kf = keys.reshape(tokens, head_group, span_size).astype(jnp.float32)
    vf = values.reshape(tokens, head_group, span_size).astype(jnp.float32)
    h1 = jnp.einsum("thi,hij->thj", kf, w_one, precision=HIGH)
    h3 = jnp.einsum("thi,hij->thj", kf, w_three, precision=HIGH)
    sg = jax.nn.sigmoid(h1)
    sil = h1 * sg
    act = sil * h3
    scaled = rates[:, :, None] * vf
    g2 = jnp.einsum("thi,thj->hij", act, scaled, precision=HIGH)
    dact = jnp.einsum("thj,hij->thi", scaled, w_two, precision=HIGH)
    d1 = dact * h3 * sg * (1.0 + h1 * (1.0 - sg))
    d3 = dact * sil
    g1 = jnp.einsum("thi,thj->hij", kf, d1, precision=HIGH)
    g3 = jnp.einsum("thi,thj->hij", kf, d3, precision=HIGH)
    grads = jnp.stack([g1, g3, g2])
    weights = jnp.stack([w_one, w_three, w_two])
    columns = span_size // lax.axis_size("seq")
    first = lax.axis_index("seq") * columns
    share = sum_at_owner(grads, "seq", 3)
    own = lax.dynamic_slice_in_dim(weights, first, columns, 3)
    fresh = renorm(own, share)
    updated = collect(fresh, "seq", 3)
    qf = queries.reshape(tokens, head_group, span_size).astype(jnp.float32)
    p1 = jnp.einsum("thi,hij->thj", qf, updated[0], precision=HIGH)
    p3 = jnp.einsum("thi,hij->thj", qf, updated[1], precision=HIGH)
    outer = jnp.einsum("thi,hij->thj", p1 * jax.nn.sigmoid(p1) * p3, updated[2], precision=HIGH)
    zed = outer * head_scale[None, :, None]
    local_sq = jnp.sum(zed * zed, axis=(1, 2))
    total_sq = of_everyone(local_sq, "head")
    all_heads = head_group * lax.axis_size("head")
    ynorm = zed / jnp.sqrt(total_sq / (all_heads * span_size) + EPS)[:, None, None]
    prior_keys, prior_values = passed_along(
        (keys[tokens - WINDOW_SPAN :], values[tokens - WINDOW_SPAN :]), "seq", 1
    )
    ext_keys = jnp.concatenate([prior_keys, keys], axis=0)
    ext_values = jnp.concatenate([prior_values, values], axis=0)
    offset = lax.axis_index("seq") * tokens
    block_span = min(512, tokens)
    scale = span_size ** (-0.5)
    query_rows = queries.reshape(tokens, head_group, span_size)
    rows = jnp.arange(block_span, dtype=jnp.int32)[:, None]
    cols = jnp.arange(block_span + WINDOW_SPAN, dtype=jnp.int32)[None, :]
    outputs = []
    for index in range(tokens // block_span):
        start_offset = index * block_span
        qb = query_rows[start_offset : start_offset + block_span]
        kb = ext_keys[start_offset : start_offset + block_span + WINDOW_SPAN].reshape(
            block_span + WINDOW_SPAN, head_group, span_size
        )
        value_block = ext_values[start_offset : start_offset + block_span + WINDOW_SPAN].reshape(
            block_span + WINDOW_SPAN, head_group, span_size
        )
        scores = jnp.einsum("ihd,jhd->hij", qb, kb, preferred_element_type=jnp.float32) * scale
        allowed = (
            (cols > rows)
            & (cols <= rows + WINDOW_SPAN)
            & (offset + start_offset + cols - WINDOW_SPAN >= 0)
        )
        scores = jnp.where(allowed[None], scores, -jnp.inf)
        top = jnp.max(scores, axis=-1, keepdims=True)
        expo = jnp.exp(scores - top)
        probs = (expo / jnp.sum(expo, axis=-1, keepdims=True)).astype(jnp.bfloat16)
        outputs.append(
            jnp.einsum("hij,jhd->ihd", probs, value_block, preferred_element_type=jnp.float32)
        )
    attn = jnp.concatenate(outputs, axis=0)
    mixed = (attn + ynorm).reshape(tokens, width)
    return (mixed, updated[0], updated[1], updated[2])


def solution(mesh):
    placed = (
        P("seq", "head"),
        P("seq", "head"),
        P("seq", "head"),
        P("seq", "head"),
        P("head"),
        P("head", None, None),
        P("head", None, None),
        P("head", None, None),
    )
    return jax.shard_map(
        per_device,
        mesh=mesh,
        in_specs=placed,
        out_specs=(
            P("seq", "head"),
            P("head", None, None),
            P("head", None, None),
            P("head", None, None),
        ),
        check_vma=False,
    )
```

profile of v0, /device:TPU:1, one launch (start us, length us, event | category | flops | bytes accessed | tf_op | source)
XLA Modules:
  0.0 147.5 jit_solution(6571401378511724956)
XLA Ops:
  0.7 1.6 %copy.219 = bf16[1024,512]{0,1:T(8,128)(2,1)S(1)} copy(bf16[1024,512]{1,0:T(8,128)(2,1)} %param.10) | data formatting | bytes 2097152 | tf_op jit(solution)/shard_map/reshape | solution.py:111
  4.8 3.4 %fusion.22 = f32[2,1024,256]{2,1,0:T(8,128)S(1)} fusion(f32[2,256,256]{2,1,0:T(8,128)S(1)} %copy-done.6, bf16[1024,2,256]{0,2,1:T(8,128)(2,1)S(1)} %bitcast.167, f32[1024,2]{0,1:T(2,128)S(1)} %copy-done.10), kind=kOutput, calls=%fused_computation.37 | convolution fusion | flops 1611661312 | bytes 3678208 | tf_op jit(solution)/shard_map/thj,hij->thi/dot_general | solution.py:71
  8.2 2.7 %fusion.39 = f32[1,2,256,32,8]{2,4,3,1,0:T(8,128)S(1)} fusion(bf16[1024,2,256]{0,2,1:T(8,128)(2,1)S(1)} %bitcast.168, f32[2,256,1024]{1,2,0:T(8,128)S(1)} %fusion.49, f32[1024,2]{0,1:T(2,128)S(1)} %copy-done.10, f32[2,256,1024]{1,2,0:T(8,128)S(1)} %fusion.47), kind=kOutput, calls=%fused_computation.60 | convolution fusion | flops 1614282752 | bytes 5775360 | tf_op jit(solution)/shard_map/thi,thj->hij/dot_general | solution.py:70
  10.9 2.0 %fusion.40 = f32[1,2,256,32,8]{2,4,3,1,0:T(8,128)S(1)} fusion(f32[2,1024,256]{2,1,0:T(8,128)S(1)} %fusion.22, bf16[128,2,8,256]{3,2,1,0:T(8,128)(2,1)S(1)} %bitcast.157, f32[2,256,1024]{1,2,0:T(8,128)S(1)} %fusion.47), kind=kOutput, calls=%fused_computation.61 | convolution fusion | flops 1613234176 | bytes 5767168 | tf_op jit(solution)/shard_map/thi,thj->hij/dot_general | solution.py:75
  13.0 2.5 %fusion.36 = f32[1,2,256,32,8]{2,4,3,1,0:T(8,128)S(1)} fusion(f32[2,256,1024]{1,2,0:T(8,128)S(1)} %fusion.47, f32[2,256,1024]{1,2,0:T(8,128)S(1)} %fusion.49, f32[2,1024,256]{2,1,0:T(8,128)S(1)} %fusion.22, bf16[128,2,8,256]{3,2,1,0:T(8,128)(2,1)S(1)} %bitcast.158), kind=kOutput, calls=%fused_computation.59 | convolution fusion | flops 1615331328 | bytes 7864320 | tf_op jit(solution)/shard_map/thi,thj->hij/dot_general | solution.py:74
  15.5 1.4 copy_bitcast_fusion
  16.9 12.1 %all-to-all-start = ((f32[32,3,2,256,8]{3,4,2,1,0:T(8,128)}), f32[32,3,2,256,8]{3,4,2,1,0:T(8,128)}, u32[]{:S(2)}, u32[]{:S(2)}) async-start(f32[32,3,2,256,8]{3,4,2,1,0:T(8,128)} %copy_bitcast_fusion), calls=%async_computation | async-start | bytes 3145728 | tf_op jit(solution)/shard_map/all_to_all | solution.py:21
  29.8 3.9 %collective-permute-start = (bf16[512,512]{1,0:T(8,128)(2,1)}, bf16[512,512]{1,0:T(8,128)(2,1)}, u32[]{:S(2)}, u32[]{:S(2)}) collective-permute-start(bf16[512,512]{1,0:T(8,128)(2,1)} %slice.39), channel_id=1, source_target_pairs={{0,8},{8,16},{16,24},{24,32},{32,40},{40,48},{48,56},{56,64},{64,7... | collective-permute-start | bytes 1572872 | tf_op jit(solution)/shard_map/ppermute | solution.py:48
  35.1 3.1 %collective-permute-start.1 = (bf16[512,512]{0,1:T(8,128)(2,1)}, bf16[512,512]{0,1:T(8,128)(2,1)}, u32[]{:S(2)}, u32[]{:S(2)}) collective-permute-start(bf16[512,512]{0,1:T(8,128)(2,1)} %slice.50), channel_id=1, source_target_pairs={{0,8},{8,16},{16,24},{24,32},{32,40},{40,48},{48,56},{56,64},{64,7... | collective-permute-start | bytes 1572872 | tf_op jit(solution)/shard_map/ppermute | solution.py:48
  38.1 2.0 %copy.171 = f32[2,256,256]{1,2,0:T(8,128)} copy(f32[2,256,256]{2,1,0:T(8,128)} %param.15) | data formatting | bytes 1048576 | tf_op args[7]
  40.2 2.1 %copy.170 = f32[2,256,256]{1,2,0:T(8,128)} copy(f32[2,256,256]{2,1,0:T(8,128)} %param.14) | data formatting | bytes 1048576 | tf_op args[6]
  42.2 2.1 %copy.169 = f32[2,256,256]{1,2,0:T(8,128)} copy(f32[2,256,256]{2,1,0:T(8,128)} %param.13) | data formatting | bytes 1048576 | tf_op args[5]
  45.3 2.0 %copy.218 = bf16[512,512]{0,1:T(8,128)(2,1)} copy(bf16[512,512]{1,0:T(8,128)(2,1)} %get-tuple-element.32) | data formatting | bytes 1048576
  47.4 2.0 %copy.217 = bf16[512,512]{0,1:T(8,128)(2,1)} copy(bf16[512,512]{1,0:T(8,128)(2,1)} %get-tuple-element.31) | data formatting | bytes 1048576
  50.3 15.6 %all-to-all-done = f32[32,3,2,256,8]{3,4,2,1,0:T(8,128)} async-done(((f32[32,3,2,256,8]{3,4,2,1,0:T(8,128)}), f32[32,3,2,256,8]{3,4,2,1,0:T(8,128)}, u32[]{:S(2)}, u32[]{:S(2)}) %all-to-all-start) | async-done | bytes 1572896 | tf_op jit(solution)/shard_map/all_to_all | solution.py:21
  65.9 1.5 %reduce_sum.65 = f32[3,2,256,8]{2,3,1,0:T(8,128)S(1)} reduce(f32[32,3,2,256,8]{3,4,2,1,0:T(8,128)} %all-to-all-done, f32[]{:T(128)} %constant.10.clone.1), dimensions={0}, to_apply=%region_4.0 | reduce | flops 380928 | bytes 1622020 | tf_op jit(solution)/shard_map/reduce_sum | solution.py:22
  67.6 1.3 broadcast_in_dim.40
  68.9 7.5 %all-to-all-start.1 = ((f32[32,3,2,256,8]{3,4,2,1,0:T(8,128)}), f32[32,3,2,256,8]{3,4,2,1,0:T(8,128)}, u32[]{:S(2)}, u32[]{:S(2)}) async-start(f32[32,3,2,256,8]{3,4,2,1,0:T(8,128)} %broadcast_in_dim.40), calls=%async_computation.1 | async-start | bytes 3145728 | tf_op jit(solution)/shard_map/all_to_all | solution.py:33
  76.5 1.7 %fusion.33 = (pred[512,1024]{0,1:T(8,128)(4,1)}, pred[512,1024]{0,1:T(8,128)(4,1)S(1)}) fusion(s32[512]{0:T(512)S(1)} %iota_add_fusion, pred[1024]{0:T(1024)(128)(4,1)S(1)} %get-tuple-element.42, pred[1024]{0:T(1024)(128)(4,1)S(1)} %get-tuple-element.41), kind=kLoop, calls=%fused_computation.50 | loop fusion | flops 2621440 | bytes 1052672 | tf_op jit(solution)/shard_map/and | solution.py:116
  78.2 1.7 %fusion.51 = f32[2,512,1024]{1,2,0:T(8,128)S(1)} fusion(bf16[512,2,256]{0,2,1:T(8,128)(2,1)} %bitcast.173, bf16[128,2,8,256]{3,2,1,0:T(8,128)(2,1)S(1)} %bitcast.159), kind=kOutput, calls=%fused_computation.72 | convolution fusion | flops 536870912 | bytes 5767168 | tf_op jit(solution)/shard_map/ihd,jhd->hij/dot_general | solution.py:114
  80.0 2.4 %fusion.78 = (f32[2,512]{1,0:T(2,128)S(1)}, f32[2,512,1024]{1,2,0:T(8,128)S(1)}) fusion(f32[2,512,1024]{1,2,0:T(8,128)S(1)} %fusion.51, pred[512,1024]{0,1:T(8,128)(4,1)S(1)} %get-tuple-element.34), kind=kOutput, calls=%fused_computation.110 | output fusion | flops 6292479 | bytes 8916992 | tf_op jit(solution)/shard_map/sub | solution.py:122
  82.4 1.8 %fusion.34 = f32[512,2,256]{0,2,1:T(8,128)} fusion(bf16[1024,2,256]{0,2,1:T(8,128)(2,1)S(1)} %bitcast.169, f32[2,512,1024]{1,2,0:T(8,128)S(1)} %get-tuple-element.36, f32[2,512]{1,0:T(2,128)S(1)} %get-tuple-element.35), kind=kOutput, calls=%fused_computation.57 | convolution fusion | flops 538968064 | bytes 6295552 | tf_op jit(solution)/shard_map/hij,jhd->ihd/dot_general | solution.py:125
  86.6 2.2 %pad_maximum_fusion.1 = bf16[1024,512]{0,1:T(8,128)(2,1)} fusion(bf16[1024,512]{0,1:T(8,128)(2,1)S(1)} %copy.156, bf16[512,512]{0,1:T(8,128)(2,1)} %collective-permute-done.1), kind=kLoop, calls=%fused_computation.74 | loop fusion | flops 2097152 | bytes 2621440 | tf_op jit(solution)/shard_map/concatenate | solution.py:96
  88.8 5.3 %fusion.79 = (f32[2,512]{1,0:T(2,128)S(1)}, f32[2,512,1024]{1,2,0:T(8,128)}) fusion(pred[512,1024]{0,1:T(8,128)(4,1)} %get-tuple-element.33, bf16[1024,2,256]{0,2,1:T(8,128)(2,1)} %bitcast.175, bf16[512,2,256]{0,2,1:T(8,128)(2,1)} %bitcast.176), kind=kOutput, calls=%fused_computation.111 | convolution fusion | flops 541066240 | bytes 6295552 | tf_op jit(solution)/shard_map/sub | solution.py:122
  94.1 3.9 %fusion.35 = f32[512,2,256]{0,2,1:T(8,128)} fusion(bf16[1024,2,256]{0,2,1:T(8,128)(2,1)S(1)} %bitcast.174, f32[2,512,1024]{1,2,0:T(8,128)} %get-tuple-element.38, f32[2,512]{1,0:T(2,128)S(1)} %get-tuple-element.37), kind=kOutput, calls=%fused_computation.58 | convolution fusion | flops 538968064 | bytes 6295552 | tf_op jit(solution)/shard_map/hij,jhd->ihd/dot_general | solution.py:125
  98.0 19.3 %all-to-all-done.1 = f32[32,3,2,256,8]{3,4,2,1,0:T(8,128)} async-done(((f32[32,3,2,256,8]{3,4,2,1,0:T(8,128)}), f32[32,3,2,256,8]{3,4,2,1,0:T(8,128)}, u32[]{:S(2)}, u32[]{:S(2)}) %all-to-all-start.1) | async-done | bytes 1572896 | tf_op jit(solution)/shard_map/all_to_all | solution.py:33
  117.3 1.5 %copy.252 = f32[32,3,2,256,8]{3,4,0,2,1:T(8,128)S(1)} copy(f32[32,3,2,256,8]{3,4,2,1,0:T(8,128)} %all-to-all-done.1) | data formatting | bytes 3145728 | tf_op jit(solution)/shard_map/all_to_all | solution.py:33
  121.0 3.8 %multiply_reduce_fusion = (f32[1024]{0:T(1024)S(1)}, f32[2,256,1024]{2,1,0:T(8,128)}) fusion(f32[2]{0:T(128)S(1)} %copy-done.11, f32[2,256,1024]{1,2,0:T(8,128)S(1)} %fusion.41, f32[2,256,1024]{1,2,0:T(8,128)S(1)} %fusion.43, f32[3,2,256,32,8]{2,4,3,1,0:T(8,128)S(1)} %bitcast.162), kind=kOutput, calls=%fused_computation.34 | convolution fusion | flops 1614806016 | bytes 6820352 | tf_op jit(solution)/shard_map/thi,hij->thj/dot_general | solution.py:87
  125.4 12.7 %all-to-all-start.2 = ((f32[8,1,1024]{2,1,0:T(1,128)}), f32[8,1,1024]{2,1,0:T(1,128)S(1)}, u32[]{:S(2)}, u32[]{:S(2)}) async-start(f32[8,1,1024]{2,1,0:T(1,128)} %broadcast_in_dim.41), calls=%async_computation.2 | async-start | bytes 65536 | tf_op jit(solution)/shard_map/all_to_all | solution.py:33
  141.4 1.5 %all-to-all-done.2 = f32[8,1,1024]{2,1,0:T(1,128)S(1)} async-done(((f32[8,1,1024]{2,1,0:T(1,128)}), f32[8,1,1024]{2,1,0:T(1,128)S(1)}, u32[]{:S(2)}, u32[]{:S(2)}) %all-to-all-start.2) | async-done | bytes 32800 | tf_op jit(solution)/shard_map/all_to_all | solution.py:33
  142.9 2.7 %maximum_add_fusion = f32[1024,2,256]{0,2,1:T(8,128)S(1)} fusion(f32[512,2,256]{0,2,1:T(8,128)} %fusion.34, f32[512,2,256]{0,2,1:T(8,128)} %fusion.35, f32[2,256,1024]{2,1,0:T(8,128)} %get-tuple-element.40, f32[1024]{0:T(1024)S(1)} %add_sqrt_fusion, f32[2]{0:T(128)S(1)} %copy-done.11), kind=kLoop, calls=%fused_computation.10 | loop fusion | flops 2097152 | bytes 6295560 | tf_op jit(solution)/shard_map/add | solution.py:128
  145.7 1.8 %copy.194 = f32[1024,512]{1,0:T(8,128)} copy(f32[1024,512]{0,1:T(8,128)S(1)} %bitcast.166) | data formatting | bytes 4194304
  (49 shorter events, 15.1 us)
Async XLA Ops:
  0.6 1.7 %copy-start = (bf16[1024,512]{1,0:T(8,128)(2,1)S(1)}, bf16[1024,512]{1,0:T(8,128)(2,1)}, u32[]{:S(2)}) copy-start(bf16[1024,512]{1,0:T(8,128)(2,1)} %param.9) | copy-start | bytes 3145732
  0.6 1.7 %copy-start.7 = (f32[2,256,256]{2,1,0:T(8,128)S(1)}, f32[2,256,256]{2,1,0:T(8,128)}, u32[]{:S(2)}) copy-start(f32[2,256,256]{2,1,0:T(8,128)} %param.14) | copy-start | bytes 1572868
  2.3 6.0 %copy-start.4 = (bf16[1024,512]{0,1:T(8,128)(2,1)}, bf16[1024,512]{0,1:T(8,128)(2,1)S(1)}, u32[]{:S(2)}) copy-start(bf16[1024,512]{0,1:T(8,128)(2,1)S(1)} %copy.219) | copy-start | bytes 3145732
  2.3 1.4 copy-start.8
  3.7 1.1 copy-start.6
  3.7 1.1 copy-start.10
  16.9 12.1 %copy-start.2 = (bf16[1024,512]{1,0:T(8,128)(2,1)S(1)}, bf16[1024,512]{1,0:T(8,128)(2,1)}, u32[]{:S(2)}) copy-start(bf16[1024,512]{1,0:T(8,128)(2,1)} %param.10) | copy-start | bytes 3145732
  16.9 49.0 %all-to-all-start = ((f32[32,3,2,256,8]{3,4,2,1,0:T(8,128)}), f32[32,3,2,256,8]{3,4,2,1,0:T(8,128)}, u32[]{:S(2)}, u32[]{:S(2)}) async-start(f32[32,3,2,256,8]{3,4,2,1,0:T(8,128)} %copy_bitcast_fusion), calls=%async_computation | async-start | bytes 3145728 | tf_op jit(solution)/shard_map/all_to_all | solution.py:21
  29.8 54.3 %collective-permute-start = (bf16[512,512]{1,0:T(8,128)(2,1)}, bf16[512,512]{1,0:T(8,128)(2,1)}, u32[]{:S(2)}, u32[]{:S(2)}) collective-permute-start(bf16[512,512]{1,0:T(8,128)(2,1)} %slice.39), channel_id=1, source_target_pairs={{0,8},{8,16},{16,24},{24,32},{32,40},{40,48},{48,56},{56,64},{64,7... | collective-permute-start | bytes 1572872 | tf_op jit(solution)/shard_map/ppermute | solution.py:48
  34.2 10.1 %copy-start.1 = (bf16[1024,512]{1,0:T(8,128)(2,1)S(1)}, bf16[1024,512]{1,0:T(8,128)(2,1)}, u32[]{:S(2)}) copy-start(bf16[1024,512]{1,0:T(8,128)(2,1)} %param.8) | copy-start | bytes 3145732
  35.1 51.5 %collective-permute-start.1 = (bf16[512,512]{0,1:T(8,128)(2,1)}, bf16[512,512]{0,1:T(8,128)(2,1)}, u32[]{:S(2)}, u32[]{:S(2)}) collective-permute-start(bf16[512,512]{0,1:T(8,128)(2,1)} %slice.50), channel_id=1, source_target_pairs={{0,8},{8,16},{16,24},{24,32},{32,40},{40,48},{48,56},{56,64},{64,7... | collective-permute-start | bytes 1572872 | tf_op jit(solution)/shard_map/ppermute | solution.py:48
  68.9 48.4 %all-to-all-start.1 = ((f32[32,3,2,256,8]{3,4,2,1,0:T(8,128)}), f32[32,3,2,256,8]{3,4,2,1,0:T(8,128)}, u32[]{:S(2)}, u32[]{:S(2)}) async-start(f32[32,3,2,256,8]{3,4,2,1,0:T(8,128)} %broadcast_in_dim.40), calls=%async_computation.1 | async-start | bytes 3145728 | tf_op jit(solution)/shard_map/all_to_all | solution.py:33
  80.0 2.4 %copy-start.5 = (bf16[1024,512]{0,1:T(8,128)(2,1)S(1)}, bf16[1024,512]{0,1:T(8,128)(2,1)}, u32[]{:S(2)}) copy-start(bf16[1024,512]{0,1:T(8,128)(2,1)} %copy-done.4) | copy-start | bytes 3145732
  82.4 1.8 %copy-start.3 = (bf16[1024,512]{1,0:T(8,128)(2,1)S(1)}, bf16[1024,512]{1,0:T(8,128)(2,1)}, u32[]{:S(2)}) copy-start(bf16[1024,512]{1,0:T(8,128)(2,1)} %param.10) | copy-start | bytes 3145732
  88.8 5.3 %copy-start.9 = (bf16[1024,512]{0,1:T(8,128)(2,1)S(1)}, bf16[1024,512]{0,1:T(8,128)(2,1)}, u32[]{:S(2)}) copy-start(bf16[1024,512]{0,1:T(8,128)(2,1)} %copy.155) | copy-start | bytes 3145732
  119.9 1.1 copy-start.11
  125.4 17.5 %all-to-all-start.2 = ((f32[8,1,1024]{2,1,0:T(1,128)}), f32[8,1,1024]{2,1,0:T(1,128)S(1)}, u32[]{:S(2)}, u32[]{:S(2)}) async-start(f32[8,1,1024]{2,1,0:T(1,128)} %broadcast_in_dim.41), calls=%async_computation.2 | async-start | bytes 65536 | tf_op jit(solution)/shard_map/all_to_all | solution.py:33
where the time goes:
time: 149 us; the launch traced here: 148 us
  starting transfers between devices  39.4 us (26%)
  waiting for transfers between devices  36.4 us (24%)
  matrix products  31.3 us (21%)
  local copies, waits for them, and re-layouts  25.3 us (17%)
  other arithmetic  14.2 us (10%)
    all_to_all x2, waiting for transfers between devices, from_everyone(): return lax.all_to_all(copies, axis, split_axis=0, concat_axis=0, tiled=True)  20.9 us
    all_to_all x2, starting transfers between devices, from_everyone(): return lax.all_to_all(copies, axis, split_axis=0, concat_axis=0, tiled=True)  20.3 us
    unnamed x34, local copies, waits for them, and re-layouts  16 us
    all_to_all x1, waiting for transfers between devices, sum_at_owner(): lax.all_to_all(pieces, axis, split_axis=0, concat_axis=0, tiled=True)  15.6 us
    all_to_all x1, starting transfers between devices, sum_at_owner(): lax.all_to_all(pieces, axis, split_axis=0, concat_axis=0, tiled=True)  12.1 us
    ppermute x2, starting transfers between devices, passed_along(): return lax.ppermute(block, axis, route)  6.96 us
    dot_general x2, matrix products, per_device(): jnp.einsum('hij,jhd->ihd', probs, value_block, preferred_element_type=jnp...  5.62 us
    sub x1, matrix products, per_device(): expo = jnp.exp(scores - top)  5.29 us
  transfers between devices with their start and end apart: 5, of which 3 were waited for; matrix products, arithmetic and copies ran while one was open for 28% of the time, Pallas kernels for 0%

commit v1 on v0

v1 whole, which is shorter than its diff:
```python
import jax
import jax.numpy as jnp
from jax import lax
from jax.experimental import pallas as pl
from jax.experimental.pallas import tpu as pltpu
from jax.sharding import PartitionSpec as P

WINDOW = 512
EPS = 1e-06
F32 = jnp.float32
BF16 = jnp.bfloat16
MESH = pl.DeviceIdType.MESH
XS, ZS, HS = 4, 8, 8
TOK, FEAT, BLK = 1024, 256, 256
NT = (((1,), (1,)), ((), ()))
NN = (((1,), (0,)), ((), ()))


def mm(a, b, dims):
    return lax.dot_general(a, b, dims, preferred_element_type=F32)


def split(x):
    hi = x.astype(BF16)
    return hi, (x - hi.astype(F32)).astype(BF16)


def cols(h):
    return pl.ds(h * FEAT, FEAT)


def layer(
    q_hbm, k_hbm, v_hbm, rate_hbm, hscale, w1_hbm, w3_hbm, w2_hbm,
    mixed_hbm, n1_hbm, n3_hbm, n2_hbm,
    q, kx, vx, rate, w, wt, wb, dt, g, rx, sx, rz, nt, nb, nout, z, out, sq,
    in_sem, out_sem, halo_s, halo_r, xs_s, xs_r, zs_s, zs_r, za_s, za_r, xa_s, xa_r, sq_s, sq_r,
):
    s = lax.axis_index("seq")
    me_h = lax.axis_index("head")
    x = s // ZS
    zz = s % ZS

    def x_peer(d):
        return ((x + d) % XS) * ZS + zz

    def z_peer(d):
        return x * ZS + (zz + d) % ZS

    barrier = pltpu.get_barrier_semaphore()
    greeted = 0
    for d in range(1, XS):
        pl.semaphore_signal(barrier, inc=1, device_id={"seq": x_peer(d)}, device_id_type=MESH)
        greeted += 1
    for d in range(1, ZS):
        pl.semaphore_signal(barrier, inc=1, device_id={"seq": z_peer(d)}, device_id_type=MESH)
        greeted += 1
    for d in range(1, HS):
        pl.semaphore_signal(barrier, inc=1, device_id={"head": (me_h + d) % HS}, device_id_type=MESH)
        greeted += 1
    after = (s + 1) % (XS * ZS)
    for peer in (after, (s + XS * ZS - 1) % (XS * ZS)):
        pl.semaphore_signal(barrier, inc=1, device_id={"seq": peer}, device_id_type=MESH)
        greeted += 1

    def fetch(src, dst, i):
        copy = pltpu.make_async_copy(src, dst, in_sem.at[i])
        copy.start()
        return copy

    loads = [
        fetch(k_hbm, kx.at[pl.ds(WINDOW, TOK), :], 0),
        fetch(v_hbm, vx.at[pl.ds(WINDOW, TOK), :], 1),
        fetch(w1_hbm, w.at[0], 2),
        fetch(w3_hbm, w.at[1], 3),
        fetch(w2_hbm, w.at[2], 4),
        fetch(rate_hbm, rate, 5),
        fetch(q_hbm, q, 6),
    ]
    for load in loads[2:5]:
        load.wait()
    for h in range(2):
        for m in range(3):
            wt[h, m] = w[m, h].T
        for m in range(2):
            hi, lo = split(wt[h, m])
            wb[h, m, 0] = hi
            wb[h, m, 1] = lo
        hi, lo = split(w[2, h])
        wb[h, 2, 0] = hi
        wb[h, 2, 1] = lo
    for load in loads[:2] + loads[5:]:
        load.wait()

    def gradients(h):
        @pl.loop(0, TOK // BLK)
        def _(i):
            start = pl.multiple_of(i * BLK, BLK)
            kt = kx[pl.ds(WINDOW + start, BLK), cols(h)]
            vt = vx[pl.ds(WINDOW + start, BLK), cols(h)]
            h1 = mm(wb[h, 0, 0], kt, NT) + mm(wb[h, 0, 1], kt, NT)
            h3 = mm(wb[h, 1, 0], kt, NT) + mm(wb[h, 1, 1], kt, NT)
            da = mm(wb[h, 2, 0], vt, NT) + mm(wb[h, 2, 1], vt, NT)
            r = rate[pl.ds(h, 1), pl.ds(start, BLK)]
            da = da * r
            sg = jax.nn.sigmoid(h1)
            sil = h1 * sg
            d1 = da * h3 * sg * (1.0 + h1 * (1.0 - sg))
            d3 = da * sil
            act = sil * h3 * r
            for n, value in enumerate((d1, d3, act)):
                hi, lo = split(value)
                dt[2 * n, :, pl.ds(start, BLK)] = hi
                dt[2 * n + 1, :, pl.ds(start, BLK)] = lo

        kh = kx[pl.ds(WINDOW, TOK), cols(h)]
        vh = vx[pl.ds(WINDOW, TOK), cols(h)]
        g[h, 0] = mm(dt[0], kh, NN) + mm(dt[1], kh, NN)
        g[h, 1] = mm(dt[2], kh, NN) + mm(dt[3], kh, NN)
        g[h, 2] = (mm(dt[4], vh, NN) + mm(dt[5], vh, NN)).T

    def remote(src, dst, send, recv, peer):
        return pltpu.make_async_remote_copy(
            src_ref=src, dst_ref=dst, send_sem=send, recv_sem=recv, device_id=peer, device_id_type=MESH
        )

    def start(copies):
        for copy in copies:
            copy.start()

    def halo(h):
        return [
            remote(
                ref.at[pl.ds(TOK, WINDOW), cols(h)],
                ref.at[pl.ds(0, WINDOW), cols(h)],
                halo_s.at[h, n],
                halo_r.at[h, n],
                {"seq": after},
            )
            for n, ref in enumerate((kx, vx))
        ]

    def reduce_x(h):
        return [
            remote(
                g.at[h, :, pl.ds(pl.multiple_of(((x + d) % XS) * 64, 64), 64), :],
                rx.at[h, d - 1],
                xs_s.at[h, d - 1],
                xs_r.at[h, d - 1],
                {"seq": x_peer(d)},
            )
            for d in range(1, XS)
        ]

    def reduce_z(h):
        return [
            remote(
                sx.at[h, :, pl.ds(pl.multiple_of(((zz + d) % ZS) * 8, 8), 8), :],
                rz.at[h, d - 1],
                zs_s.at[h, d - 1],
                zs_r.at[h, d - 1],
                {"seq": z_peer(d)},
            )
            for d in range(1, ZS)
        ]

    def gather_z(h):
        part = nt.at[h, :, pl.ds(pl.multiple_of(s * 8, 8), 8), :]
        return [
            remote(part, part, za_s.at[h, d - 1], za_r.at[h, d - 1], {"seq": z_peer(d)})
            for d in range(1, ZS)
        ]

    def gather_x(h):
        part = nt.at[h, :, pl.ds(pl.multiple_of(x * 64, 64), 64), :]
        return [
            remote(part, part, xa_s.at[h, d - 1], xa_r.at[h, d - 1], {"seq": x_peer(d)})
            for d in range(1, XS)
        ]

    def attend(h, b):
        begin = pl.multiple_of(b * BLK, BLK)
        span = BLK + WINDOW
        lanes = pl.ds(pl.multiple_of(h * FEAT, FEAT), FEAT)
        scores = mm(q[pl.ds(begin, BLK), lanes], kx[pl.ds(begin, span), lanes], NT) * (FEAT ** -0.5)
        rows = lax.broadcasted_iota(jnp.int32, (BLK, span), 0)
        keys = lax.broadcasted_iota(jnp.int32, (BLK, span), 1)
        first = jnp.where(s == 0, WINDOW - begin, 0)
        allowed = (keys > rows) & (keys <= rows + WINDOW) & (keys >= first)
        scores = jnp.where(allowed, scores, -jnp.inf)
        top = jnp.max(scores, axis=1, keepdims=True)
        expo = jnp.exp(scores - top)
        probs = (expo / jnp.sum(expo, axis=1, keepdims=True)).astype(BF16)
        out[pl.ds(begin, BLK), lanes] = mm(probs, vx[pl.ds(begin, span), lanes], NN)

    gradients(0)
    pl.semaphore_wait(barrier, greeted)
    halos = [halo(0), halo(1)]
    rxs = [reduce_x(0), reduce_x(1)]
    rzs = [reduce_z(0), reduce_z(1)]
    gzs = [gather_z(0), gather_z(1)]
    gxs = [gather_x(0), gather_x(1)]
    start(rxs[0])
    start(halos[0])
    gradients(1)
    start(rxs[1])

    @pl.loop(0, 4)
    def _(i):
        attend(i // 2, 2 + i % 2)

    def x_sum(h):
        for copy in rxs[h]:
            copy.wait_recv()
        own = g[h, :, pl.ds(pl.multiple_of(x * 64, 64), 64), :]
        sx[h] = own + rx[h, 0] + rx[h, 1] + rx[h, 2]
        start(rzs[h])

    x_sum(0)
    for copy in halos[0]:
        copy.wait_recv()

    @pl.loop(0, 2)
    def _(i):
        attend(0, i)

    x_sum(1)

    mine = pl.ds(pl.multiple_of(s * 8, 8), 8)

    def renorm(h):
        for copy in rzs[h]:
            copy.wait_recv()
        total = sx[h, :, pl.ds(pl.multiple_of(zz * 8, 8), 8), :]
        for d in range(ZS - 1):
            total = total + rz[h, d]
        weight = wt[h, :, mine, :]
        upd = weight + total
        old = jnp.sqrt(jnp.sum(weight * weight, axis=2, keepdims=True) + EPS)
        cur = jnp.sqrt(jnp.sum(upd * upd, axis=2, keepdims=True) + EPS)
        nt[h, :, mine, :] = upd * (old / cur)
        start(gzs[h])

    renorm(0)
    renorm(1)
    start(halos[1])
    for h in range(2):
        for copy in gzs[h]:
            copy.wait_recv()
        start(gxs[h])

    def final(h):
        for copy in gxs[h]:
            copy.wait_recv()
        for m in range(3):
            hi, lo = split(nt[h, m])
            nb[m, 0] = hi
            nb[m, 1] = lo

        @pl.loop(0, TOK // BLK)
        def _(i):
            begin = pl.multiple_of(i * BLK, BLK)
            qt = q[pl.ds(begin, BLK), cols(h)]
            p1 = mm(qt, nb[0, 0], NT) + mm(qt, nb[0, 1], NT)
            p3 = mm(qt, nb[1, 0], NT) + mm(qt, nb[1, 1], NT)
            hi, lo = split(p1 * jax.nn.sigmoid(p1) * p3)
            o = mm(hi, nb[2, 0], NT) + mm(lo, nb[2, 0], NT) + mm(hi, nb[2, 1], NT)
            z[pl.ds(begin, BLK), cols(h)] = o * hscale[h]

    final(0)
    final(1)

    lane = lax.broadcasted_iota(jnp.int32, (128, 128), 1)
    packed = jnp.zeros((128, 128), F32)
    for r in range(TOK // 128):
        zt = z[pl.ds(r * 128, 128), :]
        packed = jnp.where(lane == r, jnp.sum(zt * zt, axis=1, keepdims=True), packed)
    sq[0] = packed.T[:8, :]
    sqs = [
        remote(sq.at[0], sq.at[d], sq_s.at[d - 1], sq_r.at[d - 1], {"head": (me_h + d) % HS})
        for d in range(1, HS)
    ]
    start(sqs)

    news = []
    for h in range(2):
        for m, ref in enumerate((n1_hbm, n3_hbm, n2_hbm)):
            nout[h, m] = nt[h, m].T
            copy = pltpu.make_async_copy(nout.at[h, m], ref.at[h], out_sem.at[8 + 3 * h + m])
            copy.start()
            news.append(copy)

    for copy in halos[1]:
        copy.wait_recv()

    @pl.loop(0, 2)
    def _(i):
        attend(1, i)

    for copy in sqs:
        copy.wait_recv()
    total = sq[0]
    for d in range(1, HS):
        total = total + sq[d]
    inv = 1.0 / jnp.sqrt(total / (2 * HS * FEAT) + EPS)
    inv = jnp.concatenate([inv, jnp.zeros((120, 128), F32)], axis=0).T
    for r in range(TOK // 128):
        part = pl.ds(r * 128, 128)
        out[part, :] = out[part, :] + z[part, :] * inv[:, r : r + 1]
        copy = pltpu.make_async_copy(out.at[part, :], mixed_hbm.at[part, :], out_sem.at[r])
        copy.start()
        news.append(copy)
    for group in halos + rxs + rzs + gzs + gxs + [sqs]:
        for copy in group:
            copy.wait_send()
    for copy in news:
        copy.wait()


def per_device(queries, keys, values, rates, head_scale, w_one, w_three, w_two):
    any_space = pl.BlockSpec(memory_space=pl.ANY)
    dma = pltpu.SemaphoreType.DMA
    weight = jax.ShapeDtypeStruct((2, FEAT, FEAT), F32)
    return pl.pallas_call(
        layer,
        out_shape=(jax.ShapeDtypeStruct((TOK, 2 * FEAT), F32), weight, weight, weight),
        in_specs=[any_space] * 4 + [pl.BlockSpec(memory_space=pltpu.SMEM)] + [any_space] * 3,
        out_specs=(any_space,) * 4,
        scratch_shapes=[
            pltpu.VMEM((TOK, 2 * FEAT), BF16),
            pltpu.VMEM((TOK + WINDOW, 2 * FEAT), BF16),
            pltpu.VMEM((TOK + WINDOW, 2 * FEAT), BF16),
            pltpu.VMEM((2, TOK), F32),
            pltpu.VMEM((3, 2, FEAT, FEAT), F32),
            pltpu.VMEM((2, 3, FEAT, FEAT), F32),
            pltpu.VMEM((2, 3, 2, FEAT, FEAT), BF16),
            pltpu.VMEM((6, FEAT, TOK), BF16),
            pltpu.VMEM((2, 3, FEAT, FEAT), F32),
            pltpu.VMEM((2, XS - 1, 3, 64, FEAT), F32),
            pltpu.VMEM((2, 3, 64, FEAT), F32),
            pltpu.VMEM((2, ZS - 1, 3, 8, FEAT), F32),
            pltpu.VMEM((2, 3, FEAT, FEAT), F32),
            pltpu.VMEM((3, 2, FEAT, FEAT), BF16),
            pltpu.VMEM((2, 3, FEAT, FEAT), F32),
            pltpu.VMEM((TOK, 2 * FEAT), F32),
            pltpu.VMEM((TOK, 2 * FEAT), F32),
            pltpu.VMEM((HS, 8, 128), F32),
            dma((7,)),
            dma((14,)),
            dma((2, 2)),
            dma((2, 2)),
            dma((2, XS - 1)),
            dma((2, XS - 1)),
            dma((2, ZS - 1)),
            dma((2, ZS - 1)),
            dma((2, ZS - 1)),
            dma((2, ZS - 1)),
            dma((2, XS - 1)),
            dma((2, XS - 1)),
            dma((HS - 1,)),
            dma((HS - 1,)),
        ],
        compiler_params=pltpu.CompilerParams(
            collective_id=0, has_side_effects=True, vmem_limit_bytes=60 * 1024 * 1024
        ),
        name="layer",
    )(queries, keys, values, rates.T, head_scale, w_one, w_three, w_two)


def solution(mesh):
    tile = P("seq", "head")
    weight = P("head", None, None)
    return jax.shard_map(
        per_device,
        mesh=mesh,
        in_specs=(tile, tile, tile, tile, P("head"), weight, weight, weight),
        out_specs=(tile, weight, weight, weight),
        check_vma=False,
    )
```

time: 149 us -> 89.4 us (0.60)
  Pallas kernels: 0 us -> 83.1 us
  starting transfers between devices: 39.4 us -> 0 us
  waiting for transfers between devices: 36.4 us -> 0 us
  matrix products: 31.3 us -> 0 us
  local copies, waits for them, and re-layouts: 25.3 us -> 5.56 us
  other arithmetic: 14.2 us -> 0 us
    pallas_call x0 -> x1, Pallas kernels: none -> 83.1 us  [per_device(): pl.pallas_call(layer, out_shape=(jax.ShapeDtypeStruct((TOK, 2 * FEAT), F3...]
    all_to_all x3 -> x0, waiting for transfers between devices: 36.4 us -> none  [the longest x2 20.9 us: from_everyone(): return lax.all_to_all(copies, axis, split_axis=0, concat_axis=0, tiled=True)]
    all_to_all x3 -> x0, starting transfers between devices: 32.4 us -> none  [the longest x2 20.3 us: from_everyone(): return lax.all_to_all(copies, axis, split_axis=0, concat_axis=0, tiled=True)]
    dot_general x12 -> x0, matrix products: 26 us -> none  [the longest x2 5.62 us: per_device(): jnp.einsum('hij,jhd->ihd', probs, value_block, preferred_element_type=jnp...]
    unnamed x34 -> x10, local copies, waits for them, and re-layouts: 16 us -> 5.56 us
    ppermute x2 -> x0, starting transfers between devices: 6.96 us -> none  [passed_along(): return lax.ppermute(block, axis, route)]
    sub x1 -> x0, matrix products: 5.29 us -> none  [per_device(): expo = jnp.exp(scores - top)]
    slice x4 -> x0, local copies, waits for them, and re-layouts: 4 us -> none  [the longest x1 1.31 us: per_device(): ext_values[start_offset:start_offset + block_span + WINDOW_SPAN]]
  transfers between devices with their start and end apart: 5 -> 0, of which waited for: 3 -> 0; matrix products, arithmetic and copies ran while one was open for 28% -> 0% of each run, Pallas kernels for 0% -> 0%
where the time goes in v1:
time: 89.4 us; the launch traced here: 89.3 us
  Pallas kernels  83.1 us (93%)
  local copies, waits for them, and re-layouts  5.56 us (6%)
    pallas_call x1, Pallas kernels, per_device(): pl.pallas_call(layer, out_shape=(jax.ShapeDtypeStruct((TOK, 2 * FEAT), F3...  83.1 us
    unnamed x10, local copies, waits for them, and re-layouts  5.56 us

profile of v1, /device:TPU:1, one launch (start us, length us, event | category | flops | bytes accessed | tf_op | source)
XLA Modules:
  0.0 89.3 jit_solution(3110013634409962563)
XLA Ops:
  0.6 83.1 %layer.1 = (f32[1024,512]{1,0:T(8,128)}, f32[2,256,256]{2,1,0:T(8,128)}, f32[2,256,256]{2,1,0:T(8,128)}, f32[2,256,256]{2,1,0:T(8,128)}) custom-call(bf16[1024,512]{1,0:T(8,128)(2,1)} %q_hbm.1, bf16[1024,512]{1,0:T(8,128)(2,1)} %k_hbm.1, bf16[1024,512]{1,0:T(8,128)(2,1)} %v_hbm.1, f32[2,1024]{1,0:T(2,128)} %bitcast.1, f32[2]{0:T(128)} %hscale.1, ...), custom_call_target="tpu_custom_call" | custom-call | tf_op jit(solution)/shard_map/layer/pallas_call | solution.py:323
  83.8 0.0 copy-start.2
  83.8 0.0 copy-start.1
  83.8 3.2 %copy.16 = f32[1024,512]{1,0:T(8,128)} copy(f32[1024,512]{1,0:T(8,128)} %get-tuple-element.8) | data formatting | bytes 4194304
  86.9 0.0 copy-done.2
  86.9 0.0 copy-start
  86.9 0.8 copy.17
  87.7 0.0 copy-done.1
  87.7 0.8 copy.18
  88.5 0.0 copy-done
  88.5 0.8 copy.19
Async XLA Ops:
  83.8 3.2 %copy-start.2 = (f32[2,256,256]{2,1,0:T(8,128)S(1)}, f32[2,256,256]{2,1,0:T(8,128)}, u32[]{:S(2)}) copy-start(f32[2,256,256]{2,1,0:T(8,128)} %get-tuple-element.9) | copy-start | bytes 1572868
  83.8 4.0 %copy-start.1 = (f32[2,256,256]{2,1,0:T(8,128)S(1)}, f32[2,256,256]{2,1,0:T(8,128)}, u32[]{:S(2)}) copy-start(f32[2,256,256]{2,1,0:T(8,128)} %get-tuple-element.10) | copy-start | bytes 1572868
  86.9 1.6 %copy-start = (f32[2,256,256]{2,1,0:T(8,128)S(1)}, f32[2,256,256]{2,1,0:T(8,128)}, u32[]{:S(2)}) copy-start(f32[2,256,256]{2,1,0:T(8,128)} %get-tuple-element.11) | copy-start | bytes 1572868

commit v2 on v1

v2 whole, which is shorter than its diff:
```python
import jax
import jax.numpy as jnp
from jax import lax
from jax.experimental import pallas as pl
from jax.experimental.pallas import tpu as pltpu
from jax.sharding import PartitionSpec as P

WINDOW = 512
EPS = 1e-06
F32 = jnp.float32
BF16 = jnp.bfloat16
MESH = pl.DeviceIdType.MESH
scope = jax.named_scope
XS, ZS, HS = 4, 8, 8
TOK, FEAT, BLK = 1024, 256, 256
NT = (((1,), (1,)), ((), ()))
NN = (((1,), (0,)), ((), ()))


def mm(a, b, dims):
    return lax.dot_general(a, b, dims, preferred_element_type=F32)


def split(x):
    hi = x.astype(BF16)
    return hi, (x - hi.astype(F32)).astype(BF16)


def cols(h):
    return pl.ds(h * FEAT, FEAT)


LEVELS, BOTTOM = 250.0, 125.0
TINY = 1e-30


def encode(x, rate):
    code = jnp.exp2(jnp.abs(x) * rate - BOTTOM)
    return jnp.where(x < 0, -code, code)


def decode(code, step):
    code = code.astype(F32)
    value = (jnp.log2(jnp.abs(code)) + BOTTOM) * step
    return jnp.where(code < 0, -value, value)


def scale_of(x, axis):
    top = jnp.max(jnp.abs(x), axis=axis, keepdims=True) * (1.0 + 2.0 ** -6) + TINY
    return top.astype(BF16).astype(F32)


def pick_rows(rows, shape, axis):
    index = lax.broadcasted_iota(jnp.int32, shape, axis)
    return jnp.where(index == 0, rows[0], jnp.where(index == 1, rows[1], rows[2]))


def encode_root(x, old):
    code = jnp.exp2(jnp.sqrt(jnp.minimum(jnp.abs(x) / old, 1.0)) * LEVELS - BOTTOM)
    return jnp.where(x < 0, -code, code)


def decode_root(code, old):
    code = code.astype(F32)
    root = (jnp.log2(jnp.abs(code)) + BOTTOM) * (1.0 / LEVELS)
    value = root * root * old
    return jnp.where(code < 0, -value, value)


def layer(
    q_hbm, k_hbm, v_hbm, rate_hbm, hscale_hbm, w1_hbm, w3_hbm, w2_hbm,
    out, z, inv_out, nout,
    q, kx, vx, rate, hscale, w, wt, wb, old, dt, g, gc, rx, sx, sc, rz, nc, nb, sq, relay,
    in_sem, halo_s, halo_r, leg_s, leg_r, xs_s, xs_r, zs_s, zs_r, za_s, za_r, xa_s, xa_r, sq_s, sq_r,
):
    s = lax.axis_index("seq")
    me_h = lax.axis_index("head")
    x = s // ZS
    zz = s % ZS

    def x_peer(d):
        return ((x + d) % XS) * ZS + zz

    def z_peer(d):
        return x * ZS + (zz + d) % ZS

    barrier = pltpu.get_barrier_semaphore()
    greeted = 0
    for d in range(1, XS):
        pl.semaphore_signal(barrier, inc=1, device_id={"seq": x_peer(d)}, device_id_type=MESH)
        greeted += 1
    for d in range(1, ZS):
        pl.semaphore_signal(barrier, inc=1, device_id={"seq": z_peer(d)}, device_id_type=MESH)
        greeted += 1
    for d in range(1, HS):
        pl.semaphore_signal(barrier, inc=1, device_id={"head": (me_h + d) % HS}, device_id_type=MESH)
        greeted += 1
    after = (s + 1) % (XS * ZS)
    for peer in (after, (s + XS * ZS - 1) % (XS * ZS)):
        pl.semaphore_signal(barrier, inc=1, device_id={"seq": peer}, device_id_type=MESH)
        greeted += 1

    def fetch(src, dst, i):
        copy = pltpu.make_async_copy(src, dst, in_sem.at[i])
        copy.start()
        return copy

    loads = [
        fetch(w1_hbm, w.at[0], 0),
        fetch(w3_hbm, w.at[1], 1),
        fetch(w2_hbm, w.at[2], 2),
        fetch(k_hbm, kx.at[pl.ds(WINDOW, TOK), :], 3),
        fetch(v_hbm, vx.at[pl.ds(WINDOW, TOK), :], 4),
        fetch(rate_hbm, rate, 5),
        fetch(q_hbm, q, 6),
        fetch(hscale_hbm, hscale, 7),
    ]

    @pl.when(s == 0)
    def _():
        kx[pl.ds(0, WINDOW), :] = jnp.zeros((WINDOW, 2 * FEAT), BF16)
        vx[pl.ds(0, WINDOW), :] = jnp.zeros((WINDOW, 2 * FEAT), BF16)

    with scope("load_w"):
        for load in loads[:3]:
            load.wait()
    for h in range(2):
        for m in range(3):
            turned = w[m, h].T
            wt[h, m] = turned
            old[h, m] = jnp.sqrt(jnp.sum(turned * turned, axis=1, keepdims=True) + EPS)
        for m in range(2):
            hi, lo = split(wt[h, m])
            wb[h, m, 0] = hi
            wb[h, m, 1] = lo
        hi, lo = split(w[2, h])
        wb[h, 2, 0] = hi
        wb[h, 2, 1] = lo
    with scope("load_x"):
        for load in loads[3:6]:
            load.wait()

    def gradients(h):
        @pl.loop(0, TOK // BLK)
        def _(i):
            start = pl.multiple_of(i * BLK, BLK)
            kt = kx[pl.ds(WINDOW + start, BLK), cols(h)]
            vt = vx[pl.ds(WINDOW + start, BLK), cols(h)]
            h1 = mm(wb[h, 0, 0], kt, NT) + mm(wb[h, 0, 1], kt, NT)
            h3 = mm(wb[h, 1, 0], kt, NT) + mm(wb[h, 1, 1], kt, NT)
            da = mm(wb[h, 2, 0], vt, NT) + mm(wb[h, 2, 1], vt, NT)
            r = rate[pl.ds(h, 1), pl.ds(start, BLK)]
            da = da * r
            sg = jax.nn.sigmoid(h1)
            sil = h1 * sg
            d1 = da * h3 * sg * (1.0 + h1 * (1.0 - sg))
            d3 = da * sil
            act = sil * h3 * r
            for n, value in enumerate((d1, d3, act)):
                hi, lo = split(value)
                dt[2 * n, :, pl.ds(start, BLK)] = hi
                dt[2 * n + 1, :, pl.ds(start, BLK)] = lo

        kh = kx[pl.ds(WINDOW, TOK), cols(h)]
        vh = vx[pl.ds(WINDOW, TOK), cols(h)]
        g[h, 0] = mm(dt[0], kh, NN) + mm(dt[1], kh, NN)
        g[h, 1] = mm(dt[2], kh, NN) + mm(dt[3], kh, NN)
        g[h, 2] = (mm(dt[4], vh, NN) + mm(dt[5], vh, NN)).T
        scales = []
        for m in range(3):
            value = g[h, m].reshape(XS, 64, FEAT)
            scale = scale_of(value, 1)
            scales.append(scale)
            gc[h, :, pl.ds(64 * m, 64), :] = encode(value, LEVELS / scale).astype(BF16)
        gc[h, :, pl.ds(192, 8), :] = pick_rows(scales, (XS, 8, FEAT), 1).astype(BF16)

    def remote(src, dst, send, recv, peer):
        return pltpu.make_async_remote_copy(
            src_ref=src, dst_ref=dst, send_sem=send, recv_sem=recv, device_id=peer, device_id_type=MESH
        )

    def start(copies):
        for copy in copies:
            copy.start()

    def halo(h):
        return [
            remote(
                ref.at[pl.ds(TOK, WINDOW), cols(h)],
                ref.at[pl.ds(0, WINDOW), cols(h)],
                halo_s.at[h, n],
                halo_r.at[h, n],
                {"seq": after},
            )
            for n, ref in enumerate((kx, vx))
        ]

    def relay_in(h):
        return remote(
            vx.at[pl.ds(TOK, WINDOW), cols(h)], relay.at[h], leg_s.at[h], leg_r.at[h], {"seq": x_peer(1)}
        )

    def relay_out(h):
        return remote(
            relay.at[h], vx.at[pl.ds(0, WINDOW), cols(h)], halo_s.at[h, 2], halo_r.at[h, 1], {"seq": z_peer(1)}
        )

    not_last = s < XS * ZS - 1
    inner = zz < ZS - 1
    leaves = (zz == ZS - 1) & (x < XS - 1)
    relays = (zz == ZS - 1) & (x > 0)

    def send_halo(h):
        ks, vs = halo(h)

        @pl.when(not_last)
        def _():
            ks.start()

        @pl.when(inner)
        def _():
            vs.start()

    def send_leg(h):
        @pl.when(leaves)
        def _():
            relay_in(h).start()

    def send_relay(h):
        @pl.when(relays)
        def _():
            relay_in(h).wait_recv()
            relay_out(h).start()

    def await_halo(h):
        ks, vs = halo(h)

        @pl.when(s > 0)
        def _():
            ks.wait_recv()
            vs.wait_recv()

    def drain_halo(h):
        ks, vs = halo(h)

        @pl.when(not_last)
        def _():
            ks.wait_send()

        @pl.when(inner)
        def _():
            vs.wait_send()

        @pl.when(leaves)
        def _():
            relay_in(h).wait_send()

        @pl.when(relays)
        def _():
            relay_out(h).wait_send()

    def reduce_x(h):
        return [
            remote(
                gc.at[h, (x + d) % XS], rx.at[h, d - 1], xs_s.at[h, d - 1], xs_r.at[h, d - 1], {"seq": x_peer(d)}
            )
            for d in range(1, XS)
        ]

    def reduce_z(h):
        return [
            remote(
                sc.at[h, (zz + d) % ZS], rz.at[h, d - 1], zs_s.at[h, d - 1], zs_r.at[h, d - 1], {"seq": z_peer(d)}
            )
            for d in range(1, ZS)
        ]

    def gather_z(h):
        part = nc.at[h, x, zz]
        return [
            remote(part, part, za_s.at[h, d - 1], za_r.at[h, d - 1], {"seq": z_peer(d)})
            for d in range(1, ZS)
        ]

    def gather_x(h):
        part = nc.at[h, x]
        return [
            remote(part, part, xa_s.at[h, d - 1], xa_r.at[h, d - 1], {"seq": x_peer(d)})
            for d in range(1, XS)
        ]

    def attend(h, b):
        begin = pl.multiple_of(b * BLK, BLK)
        span = BLK + WINDOW
        lanes = pl.ds(pl.multiple_of(h * FEAT, FEAT), FEAT)
        scores = mm(q[pl.ds(begin, BLK), lanes], kx[pl.ds(begin, span), lanes], NT) * (FEAT ** -0.5)
        rows = lax.broadcasted_iota(jnp.int32, (BLK, span), 0)
        keys = lax.broadcasted_iota(jnp.int32, (BLK, span), 1)
        first = jnp.where(s == 0, WINDOW - begin, 0)
        allowed = (keys > rows) & (keys <= rows + WINDOW) & (keys >= first)
        scores = jnp.where(allowed, scores, -jnp.inf)
        top = jnp.max(scores, axis=1, keepdims=True)
        expo = jnp.exp(scores - top)
        probs = (expo / jnp.sum(expo, axis=1, keepdims=True)).astype(BF16)
        out[pl.ds(begin, BLK), lanes] = mm(probs, vx[pl.ds(begin, span), lanes], NN)

    with scope("greet"):
        pl.semaphore_wait(barrier, greeted)
    rxs = [reduce_x(0), reduce_x(1)]
    rzs = [reduce_z(0), reduce_z(1)]
    gzs = [gather_z(0), gather_z(1)]
    gxs = [gather_x(0), gather_x(1)]
    send_leg(0)
    send_halo(0)
    with scope("grad0"):
        gradients(0)
    start(rxs[0])
    with scope("grad1"):
        gradients(1)
    start(rxs[1])
    with scope("relay0"):
        send_relay(0)
    loads[6].wait()
    loads[7].wait()

    with scope("attn_local"):

        @pl.loop(0, 4)
        def _(i):
            attend(i // 2, 2 + i % 2)

    def x_sum(h):
        with scope(f"wait_rx{h}"):
            for copy in rxs[h]:
                copy.wait_recv()
        steps = [rx[h, d, pl.ds(192, 8), :].astype(F32) * (1.0 / LEVELS) for d in range(XS - 1)]
        codes, scales = [], []
        for m in range(3):
            total = g[h, m, pl.ds(pl.multiple_of(x * 64, 64), 64), :]
            for d in range(XS - 1):
                total = total + decode(rx[h, d, pl.ds(64 * m, 64), :], steps[d][m : m + 1, :])
            sx[h, m] = total
            scale = scale_of(total, 0)
            scales.append(scale)
            codes.append(encode(total, LEVELS / scale).reshape(ZS, 8, FEAT))
        codes.append(jnp.broadcast_to(pick_rows(scales, (8, FEAT), 0), (ZS, 8, FEAT)))
        sc[h] = jnp.concatenate(codes, axis=1).astype(BF16)
        start(rzs[h])

    x_sum(0)
    send_leg(1)
    with scope("wait_halo0"):
        await_halo(0)

    with scope("attn_h0"):

        @pl.loop(0, 2)
        def _(i):
            attend(0, i)

    x_sum(1)

    mine = pl.ds(pl.multiple_of(s * 8, 8), 8)

    def renorm(h):
        with scope(f"wait_rz{h}"):
            for copy in rzs[h]:
                copy.wait_recv()
        codes = [rz[h, d].astype(F32) for d in range(ZS - 1)]
        parts = []
        for m in range(3):
            total = sx[h, m, pl.ds(pl.multiple_of(zz * 8, 8), 8), :]
            for code in codes:
                total = total + decode(code[8 * m : 8 * m + 8, :], code[24 + m : 25 + m, :] * (1.0 / LEVELS))
            upd = wt[h, m, mine, :] + total
            was = old[h, m, mine, :]
            cur = jnp.sqrt(jnp.sum(upd * upd, axis=1, keepdims=True) + EPS)
            parts.append(encode_root(upd * (was / cur), was))
        nc[h, x, zz] = jnp.concatenate(parts, axis=0).astype(BF16)
        start(gzs[h])

    renorm(0)
    renorm(1)
    send_halo(1)
    with scope("relay1"):
        send_relay(1)
    for h in range(2):
        with scope(f"wait_gz{h}"):
            for copy in gzs[h]:
                copy.wait_recv()
        start(gxs[h])

    def final(h):
        with scope(f"wait_gx{h}"):
            for copy in gxs[h]:
                copy.wait_recv()
        for m in range(3):
            fresh = decode_root(nc[h, :, :, pl.ds(8 * m, 8), :].reshape(FEAT, FEAT), old[h, m])
            hi, lo = split(fresh)
            nb[m, 0] = hi
            nb[m, 1] = lo
            g[h, m] = fresh

        @pl.loop(0, TOK // BLK)
        def _(i):
            begin = pl.multiple_of(i * BLK, BLK)
            qt = q[pl.ds(begin, BLK), cols(h)]
            p1 = mm(qt, nb[0, 0], NT) + mm(qt, nb[0, 1], NT)
            p3 = mm(qt, nb[1, 0], NT) + mm(qt, nb[1, 1], NT)
            hi, lo = split(p1 * jax.nn.sigmoid(p1) * p3)
            o = mm(hi, nb[2, 0], NT) + mm(lo, nb[2, 0], NT) + mm(hi, nb[2, 1], NT)
            z[pl.ds(begin, BLK), cols(h)] = o * hscale[h]

    with scope("final0"):
        final(0)
    with scope("final1"):
        final(1)

    lane = lax.broadcasted_iota(jnp.int32, (128, 128), 1)
    packed = jnp.zeros((128, 128), F32)
    for r in range(TOK // 128):
        zt = z[pl.ds(r * 128, 128), :]
        packed = jnp.where(lane == r, jnp.sum(zt * zt, axis=1, keepdims=True), packed)
    sq[0] = packed.T[:8, :]
    sqs = [
        remote(sq.at[0], sq.at[d], sq_s.at[d - 1], sq_r.at[d - 1], {"head": (me_h + d) % HS})
        for d in range(1, HS)
    ]
    start(sqs)

    for h in range(2):
        for m in range(3):
            nout[m, h] = g[h, m].T

    with scope("wait_halo1"):
        await_halo(1)

    with scope("attn_h1"):

        @pl.loop(0, 2)
        def _(i):
            attend(1, i)

    with scope("wait_sq"):
        for copy in sqs:
            copy.wait_recv()
    total = sq[0]
    for d in range(1, HS):
        total = total + sq[d]
    inv = 1.0 / jnp.sqrt(total / (2 * HS * FEAT) + EPS)
    inv_out[...] = jnp.concatenate([inv, jnp.zeros((120, 128), F32)], axis=0).T
    with scope("wait_end"):
        for group in rxs + rzs + gzs + gxs + [sqs]:
            for copy in group:
                copy.wait_send()
        drain_halo(0)
        drain_halo(1)


def combine(attn, z, inv, fresh, mixed_hbm, n1_hbm, n3_hbm, n2_hbm, out, sem):
    copies = [
        pltpu.make_async_copy(fresh.at[m], ref, sem.at[8 + m])
        for m, ref in enumerate((n1_hbm, n3_hbm, n2_hbm))
    ]
    for copy in copies:
        copy.start()
    scale = inv[...]
    for r in range(TOK // 128):
        part = pl.ds(r * 128, 128)
        out[part, :] = attn[part, :] + z[part, :] * scale[:, r : r + 1]
        copy = pltpu.make_async_copy(out.at[part, :], mixed_hbm.at[part, :], sem.at[r])
        copy.start()
        copies.append(copy)
    for copy in copies:
        copy.wait()


def per_device(queries, keys, values, rates, head_scale, w_one, w_three, w_two):
    any_space = pl.BlockSpec(memory_space=pltpu.HBM)
    vmem = pl.BlockSpec(memory_space=pltpu.VMEM)
    dma = pltpu.SemaphoreType.DMA
    rows = jax.ShapeDtypeStruct((TOK, 2 * FEAT), F32)
    weight = jax.ShapeDtypeStruct((2, FEAT, FEAT), F32)
    pinned = [
        pltpu.with_memory_space_constraint(a, pltpu.HBM) for a in (queries, keys, values, rates.T, head_scale, w_one, w_three, w_two)
    ]
    attn, z, inv, fresh = pl.pallas_call(
        layer,
        out_shape=(rows, rows, jax.ShapeDtypeStruct((128, 128), F32), jax.ShapeDtypeStruct((3, 2, FEAT, FEAT), F32)),
        in_specs=[any_space] * 8,
        out_specs=(vmem,) * 4,
        scratch_shapes=[
            pltpu.VMEM((TOK, 2 * FEAT), BF16),
            pltpu.VMEM((TOK + WINDOW, 2 * FEAT), BF16),
            pltpu.VMEM((TOK + WINDOW, 2 * FEAT), BF16),
            pltpu.VMEM((2, TOK), F32),
            pltpu.SMEM((2,), F32),
            pltpu.VMEM((3, 2, FEAT, FEAT), F32),
            pltpu.VMEM((2, 3, FEAT, FEAT), F32),
            pltpu.VMEM((2, 3, 2, FEAT, FEAT), BF16),
            pltpu.VMEM((2, 3, FEAT, 1), F32),
            pltpu.VMEM((6, FEAT, TOK), BF16),
            pltpu.VMEM((2, 3, FEAT, FEAT), F32),
            pltpu.VMEM((2, XS, 200, FEAT), BF16),
            pltpu.VMEM((2, XS - 1, 200, FEAT), BF16),
            pltpu.VMEM((2, 3, 64, FEAT), F32),
            pltpu.VMEM((2, ZS, 32, FEAT), BF16),
            pltpu.VMEM((2, ZS - 1, 32, FEAT), BF16),
            pltpu.VMEM((2, XS, ZS, 24, FEAT), BF16),
            pltpu.VMEM((3, 2, FEAT, FEAT), BF16),
            pltpu.VMEM((HS, 8, 128), F32),
            pltpu.VMEM((2, WINDOW, FEAT), BF16),
            dma((8,)),
            dma((2, 3)),
            dma((2, 2)),
            dma((2,)),
            dma((2,)),
            dma((2, XS - 1)),
            dma((2, XS - 1)),
            dma((2, ZS - 1)),
            dma((2, ZS - 1)),
            dma((2, ZS - 1)),
            dma((2, ZS - 1)),
            dma((2, XS - 1)),
            dma((2, XS - 1)),
            dma((HS - 1,)),
            dma((HS - 1,)),
        ],
        compiler_params=pltpu.CompilerParams(
            collective_id=0, has_side_effects=True, vmem_limit_bytes=40 * 1024 * 1024
        ),
        name="layer",
    )(*pinned)
    return pl.pallas_call(
        combine,
        out_shape=(rows, weight, weight, weight),
        in_specs=[vmem] * 4,
        out_specs=(any_space,) * 4,
        scratch_shapes=[pltpu.VMEM((TOK, 2 * FEAT), F32), dma((11,))],
        compiler_params=pltpu.CompilerParams(vmem_limit_bytes=16 * 1024 * 1024),
        name="combine",
    )(attn, z, inv, fresh)


def solution(mesh):
    tile = P("seq", "head")
    weight = P("head", None, None)
    return jax.shard_map(
        per_device,
        mesh=mesh,
        in_specs=(tile, tile, tile, tile, P("head"), weight, weight, weight),
        out_specs=(tile, weight, weight, weight),
        check_vma=False,
    )
```

time: 89.4 us -> 61 us (0.68)
  Pallas kernels: 83.1 us -> 60.3 us
  local copies, waits for them, and re-layouts: 5.56 us -> 0 us
    pallas_call x1 -> x2, Pallas kernels: 83.1 us -> 60.3 us  [the longest x1 58.4 us: per_device(): pl.pallas_call(layer, out_shape=(rows, rows, jax.ShapeDtypeStruct((128, 1...]
    unnamed x10 -> x0, local copies, waits for them, and re-layouts: 5.56 us -> none
where the time goes in v2:
time: 61 us
  Pallas kernels  60.3 us (99%)
  between operations  0.64 us (1%)
    pallas_call x1, Pallas kernels, per_device(): pl.pallas_call(layer, out_shape=(rows, rows, jax.ShapeDtypeStruct((128, 1...  58.4 us
    pallas_call x1, Pallas kernels, per_device(): pl.pallas_call(combine, out_shape=(rows, weight, weight, weight), in_spec...  1.92 us

profile of v2, /device:TPU:1, one launch (start us, length us, event | category | flops | bytes accessed | tf_op | source)
XLA Modules:
  0.0 61.0 jit_solution(4251011970807412154)
XLA Ops:
  0.6 58.4 %layer.1 = (f32[1024,512]{1,0:T(8,128)S(1)}, f32[1024,512]{1,0:T(8,128)S(1)}, f32[128,128]{1,0:T(8,128)S(1)}, f32[3,2,256,256]{3,2,1,0:T(8,128)S(1)}) custom-call(bf16[1024,512]{1,0:T(8,128)(2,1)} %q_hbm.1, bf16[1024,512]{1,0:T(8,128)(2,1)} %k_hbm.1, bf16[1024,512]{1,0:T(8,128)(2,1)} %v_hbm.1, f32[2,1024]{1,0:T(2,128)} %bitcast.1, f32[2]{0:T(128)} %hscale_hbm.1, ...), custom_call_target="tpu_custom_call" | custom-call | tf_op jit(solution)/shard_map/layer/pallas_call | solution.py:487
  59.0 1.9 %combine.1 = (f32[1024,512]{1,0:T(8,128)}, f32[2,256,256]{2,1,0:T(8,128)}, f32[2,256,256]{2,1,0:T(8,128)}, f32[2,256,256]{2,1,0:T(8,128)}) custom-call(f32[1024,512]{1,0:T(8,128)S(1)} %get-tuple-element.8.attn, f32[1024,512]{1,0:T(8,128)S(1)} %get-tuple-element.9.z, f32[128,128]{1,0:T(8,128)S(1)} %get-tuple-element.10.inv, ...), custom_call_target="tpu_custom_call" | custom-call | tf_op jit(solution)/shard_map/combine/pallas_call | solution.py:534

commit v3 on v2

v3 whole, which is shorter than its diff:
```python
import math
import jax
import jax.numpy as jnp
from jax import lax
from jax.experimental import pallas as pl
from jax.experimental.pallas import tpu as pltpu
from jax.sharding import PartitionSpec as P

WINDOW = 512
EPS = 1e-06
F32 = jnp.float32
BF16 = jnp.bfloat16
MESH = pl.DeviceIdType.MESH
scope = jax.named_scope
XS, ZS, HS = 4, 8, 8
TOK, FEAT, BLK = 1024, 256, 256
NT = (((1,), (1,)), ((), ()))
NN = (((1,), (0,)), ((), ()))


def mm(a, b, dims):
    return lax.dot_general(a, b, dims, preferred_element_type=F32)


def split(x):
    hi = x.astype(BF16)
    return hi, (x - hi.astype(F32)).astype(BF16)


def cols(h):
    return pl.ds(h * FEAT, FEAT)


LEVELS, BOTTOM = 250.0, 125.0
SOFT = math.log2(math.e) * FEAT ** -0.5
GROUPS = ((0, (0, 1)), (0, (2,)), (1, (0, 1)), (1, (2,)))
TINY = 1e-30


def sigmoid(x):
    return 0.5 * jnp.tanh(0.5 * x) + 0.5


def encode(x, rate):
    code = jnp.exp2(jnp.abs(x) * rate - BOTTOM)
    return jnp.where(x < 0, -code, code)


def decode(code, step):
    code = code.astype(F32)
    value = (jnp.log2(jnp.abs(code)) + BOTTOM) * step
    return jnp.where(code < 0, -value, value)


def scale_of(x, axis):
    top = jnp.max(jnp.abs(x), axis=axis, keepdims=True) * (1.0 + 2.0 ** -6) + TINY
    return top.astype(BF16).astype(F32)


def pick_rows(rows, shape, axis):
    if len(rows) == 1:
        return jnp.broadcast_to(rows[0], shape)
    index = lax.broadcasted_iota(jnp.int32, shape, axis)
    return jnp.where(index == 0, rows[0], rows[1])


def encode_root(x, old):
    code = jnp.exp2(jnp.sqrt(jnp.minimum(jnp.abs(x) / old, 1.0)) * LEVELS - BOTTOM)
    return jnp.where(x < 0, -code, code)


def decode_root(code, old):
    code = code.astype(F32)
    root = (jnp.log2(jnp.abs(code)) + BOTTOM) * (1.0 / LEVELS)
    value = root * root * old
    return jnp.where(code < 0, -value, value)


def layer(
    q_hbm, k_hbm, v_hbm, rate_hbm, hscale_hbm, w1_hbm, w3_hbm, w2_hbm,
    out, z, inv_out, nout,
    q, kx, vx, rate, hscale, w, wt, wb, old, dt, g, gc, rx, sx, sc, rz, nc, nb, act, sq, kh, vh, v_relay, qh, qh0, q_relay, st, st_in, st_joint, st_back, oc, oc0, oh, oh0, o_relay,
    in_sem, hs, hr, xs_s, xs_r, zs_s, zs_r, za_s, za_r, xa_s, xa_r, sq_s, sq_r,
):
    s = lax.axis_index("seq")
    me_h = lax.axis_index("head")
    x = s // ZS
    zz = s % ZS

    def x_peer(d):
        return ((x + d) % XS) * ZS + zz

    def z_peer(d):
        return x * ZS + (zz + d) % ZS

    barrier = pltpu.get_barrier_semaphore()
    greeted = 0
    for d in range(1, XS):
        pl.semaphore_signal(barrier, inc=1, device_id={"seq": x_peer(d)}, device_id_type=MESH)
        greeted += 1
    for d in range(1, ZS):
        pl.semaphore_signal(barrier, inc=1, device_id={"seq": z_peer(d)}, device_id_type=MESH)
        greeted += 1
    for d in range(1, HS):
        pl.semaphore_signal(barrier, inc=1, device_id={"head": (me_h + d) % HS}, device_id_type=MESH)
        greeted += 1
    after = (s + 1) % (XS * ZS)
    before = (s + XS * ZS - 1) % (XS * ZS)
    for peer in (after, before):
        pl.semaphore_signal(barrier, inc=1, device_id={"seq": peer}, device_id_type=MESH)
        greeted += 1

    def fetch(src, dst, i):
        copy = pltpu.make_async_copy(src, dst, in_sem.at[i])
        copy.start()
        return copy

    def fetch_head(h):
        return [
            fetch(w1_hbm.at[h], w.at[0, h], 8 * h),
            fetch(w3_hbm.at[h], w.at[1, h], 8 * h + 1),
            fetch(w2_hbm.at[h], w.at[2, h], 8 * h + 2),
            fetch(k_hbm.at[:, cols(h)], kx.at[:, cols(h)], 8 * h + 3),
            fetch(v_hbm.at[:, cols(h)], vx.at[:, cols(h)], 8 * h + 4),
        ]

    loads = [fetch_head(0)]
    rate_load = fetch(rate_hbm, rate, 5)
    front = pl.ds(0, WINDOW)
    back = pl.ds(WINDOW, WINDOW)
    q_load = fetch(q_hbm.at[front, :], q.at[front, :], 6)
    loads.append(fetch_head(1))
    late_loads = [fetch(q_hbm.at[back, :], q.at[back, :], 13), fetch(hscale_hbm, hscale, 7)]

    def prepare(h):
        with scope(f"load{h}"):
            for load in loads[h][:3] if h == 0 else loads[h]:
                load.wait()
        for m in range(3):
            turned = w[m, h].T
            wt[h, m] = turned
            old[h, m] = jnp.sqrt(jnp.sum(turned * turned, axis=1, keepdims=True) + EPS)
        for m in range(2):
            hi, lo = split(wt[h, m])
            wb[h, m, 0] = hi
            wb[h, m, 1] = lo
        hi, lo = split(w[2, h])
        wb[h, 2, 0] = hi
        wb[h, 2, 1] = lo

    def gradients(h):
        @pl.loop(0, TOK // BLK, unroll=True)
        def _(i):
            start = pl.multiple_of(i * BLK, BLK)
            kt = kx[pl.ds(start, BLK), cols(h)]
            vt = vx[pl.ds(start, BLK), cols(h)]
            h1 = mm(wb[h, 0, 0], kt, NT) + mm(wb[h, 0, 1], kt, NT)
            h3 = mm(wb[h, 1, 0], kt, NT) + mm(wb[h, 1, 1], kt, NT)
            da = mm(wb[h, 2, 0], vt, NT) + mm(wb[h, 2, 1], vt, NT)
            r = rate[pl.ds(h, 1), pl.ds(start, BLK)]
            da = da * r
            sg = sigmoid(h1)
            sil = h1 * sg
            d1 = da * h3 * sg * (1.0 + h1 * (1.0 - sg))
            d3 = da * sil
            act = sil * h3 * r
            for n, value in enumerate((d1, d3, act)):
                hi, lo = split(value)
                dt[2 * n, :, pl.ds(start, BLK)] = hi
                dt[2 * n + 1, :, pl.ds(start, BLK)] = lo

        kh = kx[:, cols(h)]
        vh = vx[:, cols(h)]
        g[h, 0] = mm(dt[0], kh, NN) + mm(dt[1], kh, NN)
        g[h, 1] = mm(dt[2], kh, NN) + mm(dt[3], kh, NN)
        pack_share(2 * h)
        g[h, 2] = (mm(dt[4], vh, NN) + mm(dt[5], vh, NN)).T
        start(reduce_x(2 * h))
        pack_share(2 * h + 1)
        start(reduce_x(2 * h + 1))

    def pack_share(i):
        h, ms = GROUPS[i]
        scales = []
        for n, m in enumerate(ms):
            value = g[h, m].reshape(XS, 64, FEAT)
            scale = scale_of(value, 1)
            scales.append(scale)
            gc[i, :, pl.ds(64 * n, 64), :] = encode(value, LEVELS / scale).astype(BF16)
        gc[i, :, pl.ds(64 * len(ms), 8), :] = pick_rows(scales, (XS, 8, FEAT), 1).astype(BF16)

    def remote(src, dst, send, recv, peer):
        return pltpu.make_async_remote_copy(
            src_ref=src, dst_ref=dst, send_sem=send, recv_sem=recv, device_id=peer, device_id_type=MESH
        )

    def start(copies):
        for copy in copies:
            copy.start()

    last = XS * ZS - 1

    def block(n):
        return pl.ds(n * BLK, BLK)

    tail = pl.ds(TOK - BLK, BLK)

    def k_copy():
        return remote(kx.at[tail, cols(0)], kh, hs.at[0], hr.at[0], {"seq": after})

    def v_copy():
        return remote(vx.at[tail, cols(0)], vh, hs.at[1], hr.at[1], {"seq": after})

    def v_leg():
        return remote(vx.at[tail, cols(0)], v_relay, hs.at[2], hr.at[2], {"seq": x_peer(1)})

    def v_forward():
        return remote(v_relay, vh, hs.at[3], hr.at[1], {"seq": z_peer(1)})

    def query_copy():
        return remote(q.at[front, cols(1)], qh, hs.at[4], hr.at[3], {"seq": before})

    def query_leg():
        return remote(q.at[front, cols(1)], q_relay, hs.at[5], hr.at[4], {"seq": x_peer(XS - 1)})

    def query_forward():
        return remote(q_relay, qh, hs.at[6], hr.at[3], {"seq": z_peer(ZS - 1)})

    def stat_copy():
        return remote(st, st_in, hs.at[7], hr.at[5], {"seq": before})

    def attn_copy():
        return remote(oc, oh, hs.at[8], hr.at[6], {"seq": after})

    def attn_leg():
        return remote(oc, o_relay, hs.at[9], hr.at[7], {"seq": x_peer(1)})

    def attn_forward():
        return remote(o_relay, oh, hs.at[10], hr.at[6], {"seq": z_peer(1)})

    def total_copy():
        return remote(st_joint, st_back, hs.at[11], hr.at[8], {"seq": after})

    def query0_copy():
        return remote(q.at[block(0), cols(0)], qh0, hs.at[12], hr.at[9], {"seq": before})

    def attn0_copy():
        return remote(oc0, oh0, hs.at[13], hr.at[10], {"seq": after})

    low, high = zz == 0, zz == ZS - 1
    transfers = {
        "k": (s < last, k_copy),
        "v": (zz < ZS - 1, v_copy),
        "v_leg": (high & (x < XS - 1), v_leg),
        "v_forward": (high & (x > 0), v_forward),
        "query": (zz > 0, query_copy),
        "query_leg": (low & (x > 0), query_leg),
        "query_forward": (low & (x < XS - 1), query_forward),
        "stat": (s > 0, stat_copy),
        "attn": (zz < ZS - 1, attn_copy),
        "attn_leg": (high & (x < XS - 1), attn_leg),
        "attn_forward": (high & (x > 0), attn_forward),
        "total": (s < last, total_copy),
        "query0": (s > 0, query0_copy),
        "attn0": (s < last, attn0_copy),
    }

    def send(*names):
        for name in names:
            wanted, copy = transfers[name]

            @pl.when(wanted)
            def _():
                copy().start()

    def pass_on(leg, forward):
        @pl.when(transfers[forward][0])
        def _():
            leg().wait_recv()
            transfers[forward][1]().start()

    def drain_halo():
        for wanted, copy in transfers.values():

            @pl.when(wanted)
            def _():
                copy().wait_send()

    def reduce_x(i):
        rows = pl.ds(0, 64 * len(GROUPS[i][1]) + 8)
        return [
            remote(
                gc.at[i, (x + d) % XS, rows, :],
                rx.at[i, d - 1, rows, :],
                xs_s.at[i, d - 1],
                xs_r.at[i, d - 1],
                {"seq": x_peer(d)},
            )
            for d in range(1, XS)
        ]

    def reduce_z(i):
        rows = pl.ds(0, 8 * len(GROUPS[i][1]) + 8)
        return [
            remote(
                sc.at[i, (zz + d) % ZS, rows, :],
                rz.at[i, d - 1, rows, :],
                zs_s.at[i, d - 1],
                zs_r.at[i, d - 1],
                {"seq": z_peer(d)},
            )
            for d in range(1, ZS)
        ]

    def gather_z(i):
        part = nc.at[i, x, zz, pl.ds(0, 8 * len(GROUPS[i][1])), :]
        return [
            remote(part, part, za_s.at[i, d - 1], za_r.at[i, d - 1], {"seq": z_peer(d)})
            for d in range(1, ZS)
        ]

    def gather_x(i):
        part = nc.at[i, x, :, pl.ds(0, 8 * len(GROUPS[i][1])), :]
        return [
            remote(part, part, xa_s.at[i, d - 1], xa_r.at[i, d - 1], {"seq": x_peer(d)})
            for d in range(1, XS)
        ]

    def received(copies):
        for copy in copies:
            copy.wait_recv()

    tile_rows = lax.broadcasted_iota(jnp.int32, (BLK, BLK), 0)
    tile_keys = lax.broadcasted_iota(jnp.int32, (BLK, BLK), 1)

    def older(scores):
        return jnp.where(tile_keys > tile_rows, scores, -jnp.inf)

    def newer(scores):
        return jnp.where(tile_keys <= tile_rows, scores, -jnp.inf)

    def row_max(tiles):
        top = tiles[0]
        for tile in tiles[1:]:
            top = jnp.maximum(top, tile)
        return jnp.max(top, axis=1, keepdims=True)

    def row_sum(tiles):
        total = tiles[0]
        for tile in tiles[1:]:
            total = total + tile
        return jnp.sum(total, axis=1, keepdims=True)

    def expos(tiles, top):
        return [jnp.exp2((tile - top) * SOFT) for tile in tiles]

    def weigh(tiles, total, values):
        scale = 1.0 / total
        result = None
        for tile, value in zip(tiles, values):
            part = mm((tile * scale).astype(BF16), value, NN)
            result = part if result is None else result + part
        return result

    def attend(h, b):
        qt = q[block(b), cols(h)]
        tiles, values = [], []
        for i, n in enumerate((b - 2, b - 1, b)):
            tile = mm(qt, kx[block(n), cols(h)] if n >= 0 else kh[...], NT)
            if i == 0:
                tile = older(tile)
            if i == 2:
                tile = newer(tile)
            if n < 0:
                tile = jnp.where(s == 0, -jnp.inf, tile)
            tiles.append(tile)
            values.append(vx[block(n), cols(h)] if n >= 0 else vh[...])
        tiles = expos(tiles, row_max(tiles))
        out[block(b), cols(h)] = weigh(tiles, row_sum(tiles), values)

    lane = lax.broadcasted_iota(jnp.int32, (128, 128), 1)

    def to_rows(columns):
        packed = jnp.zeros((128, 128), F32)
        for n, column in enumerate(columns):
            packed = jnp.where(lane == n, column, packed)
        return packed.T

    def to_columns(rows):
        turned = jnp.concatenate([rows, jnp.zeros((112, 128), F32)], axis=0).T
        return [
            jnp.concatenate([turned[:, 2 * b : 2 * b + 1], turned[:, 2 * b + 1 : 2 * b + 2]], axis=0)
            for b in range(6)
        ]

    def halves(column):
        return [column[:128], column[128:]]

    shared = ((1, 0), (1, 1), (0, 0))

    def near_tiles(h, b):
        qt = q[block(b), cols(h)]
        tiles = [mm(qt, kx[block(n), cols(h)], NT) for n in range(b + 1)]
        tiles[b] = newer(tiles[b])
        values = [vx[block(n), cols(h)] for n in range(b + 1)]
        if h == 0:
            tiles.append(jnp.where(s == 0, -jnp.inf, mm(qt, kh[...], NT)))
            values.append(vh[...])
        return tiles, values

    def near_stats():
        tops, sums = [], []
        for h, b in shared:
            tiles, _ = near_tiles(h, b)
            top = row_max(tiles)
            tops += halves(top)
            sums += halves(row_sum(expos(tiles, top)))
        st[...] = to_rows(tops + sums)[:16]

    def await_query():
        @pl.when(s < last)
        def _():
            query0_copy().wait_recv()
            query_copy().wait_recv()
            stat_copy().wait_recv()

    def far_part():
        near = to_columns(st_in[...])
        tops, sums = [], []
        for i, (h, b) in enumerate(shared):
            qt = qh[block(b), :] if h == 1 else qh0[...]
            keys = range(2 + b, 4) if h == 1 else (2,)
            tiles = [mm(qt, kx[block(n), cols(h)], NT) for n in keys]
            tiles[0] = older(tiles[0])
            top = jnp.maximum(row_max(tiles), near[i])
            tiles = expos(tiles, top)
            total = row_sum(tiles) + near[3 + i] * jnp.exp2((near[i] - top) * SOFT)
            part = weigh(tiles, total, [vx[block(n), cols(h)] for n in keys])
            scale = scale_of(part, 0)
            code = encode(part, LEVELS / scale).astype(BF16)
            scale = jnp.broadcast_to(scale, (8, FEAT)).astype(BF16)
            if h == 1:
                oc[b, pl.ds(0, BLK), :] = code
                oc[b, pl.ds(BLK, 8), :] = scale
            else:
                oc0[pl.ds(0, BLK), :] = code
                oc0[pl.ds(BLK, 8), :] = scale
            tops += halves(top)
            sums += halves(total)
        st_joint[...] = to_rows(tops + sums)[:16]

    def near_part():
        with scope("wait_o"):

            @pl.when(s > 0)
            def _():
                attn0_copy().wait_recv()
                attn_copy().wait_recv()
                total_copy().wait_recv()

        @pl.when(s == 0)
        def _():
            st_back[...] = st[...]
            oh[...] = jnp.zeros((2, BLK + 8, FEAT), BF16)
            oh0[...] = jnp.zeros((BLK + 8, FEAT), BF16)

        joint = to_columns(st_back[...])
        for i, (h, b) in enumerate(shared):
            tiles, values = near_tiles(h, b)
            near = weigh(expos(tiles, joint[i]), joint[3 + i], values)
            code = oh[b] if h == 1 else oh0[...]
            far = decode(code[:BLK], code[BLK:].astype(F32)[:1, :] * (1.0 / LEVELS))
            out[block(b), cols(h)] = near + jnp.where(s > 0, far, 0.0)

    prepare(0)
    with scope("greet"):
        pl.semaphore_wait(barrier, greeted)
    rate_load.wait()
    q_load.wait()
    for load in loads[0][3:]:
        load.wait()
    send("k", "query_leg", "query", "v_leg", "v", "query0")
    with scope("grad0"):
        gradients(0)
    prepare(1)
    with scope("grad1"):
        gradients(1)
    with scope("forward"):
        pass_on(query_leg, "query_forward")
        pass_on(v_leg, "v_forward")
    for load in late_loads:
        load.wait()
    with scope("wait_k"):

        @pl.when(s > 0)
        def _():
            k_copy().wait_recv()

        @pl.when(s == 0)
        def _():
            kh[...] = jnp.zeros((BLK, FEAT), BF16)
            vh[...] = jnp.zeros((BLK, FEAT), BF16)

    with scope("stats"):
        near_stats()
    send("stat")

    def x_sum(i):
        h, ms = GROUPS[i]
        with scope(f"wait_rx{i}"):
            received(reduce_x(i))
        steps = [rx[i, d, pl.ds(64 * len(ms), 8), :].astype(F32) * (1.0 / LEVELS) for d in range(XS - 1)]
        codes, scales = [], []
        for n, m in enumerate(ms):
            total = g[h, m, pl.ds(pl.multiple_of(x * 64, 64), 64), :]
            for d in range(XS - 1):
                total = total + decode(rx[i, d, pl.ds(64 * n, 64), :], steps[d][n : n + 1, :])
            sx[h, m] = total
            scale = scale_of(total, 0)
            scales.append(scale)
            codes.append(encode(total, LEVELS / scale).reshape(ZS, 8, FEAT))
        codes.append(jnp.broadcast_to(pick_rows(scales, (8, FEAT), 0), (ZS, 8, FEAT)))
        sc[i, :, pl.ds(0, 8 * len(ms) + 8), :] = jnp.concatenate(codes, axis=1).astype(BF16)
        start(reduce_z(i))

    mine = pl.ds(pl.multiple_of(s * 8, 8), 8)

    def renorm(i):
        h, ms = GROUPS[i]
        with scope(f"wait_rz{i}"):
            received(reduce_z(i))
        codes = [rz[i, d, pl.ds(0, 8 * len(ms) + 8), :].astype(F32) for d in range(ZS - 1)]
        parts = []
        for n, m in enumerate(ms):
            total = sx[h, m, pl.ds(pl.multiple_of(zz * 8, 8), 8), :]
            for code in codes:
                row = 8 * len(ms) + n
                total = total + decode(code[8 * n : 8 * n + 8, :], code[row : row + 1, :] * (1.0 / LEVELS))
            upd = wt[h, m, mine, :] + total
            was = old[h, m, mine, :]
            cur = jnp.sqrt(jnp.sum(upd * upd, axis=1, keepdims=True) + EPS)
            parts.append(encode_root(upd * (was / cur), was))
        nc[i, x, zz, pl.ds(0, 8 * len(ms)), :] = jnp.concatenate(parts, axis=0).astype(BF16)
        start(gather_z(i))

    def spread(i):
        with scope(f"wait_gz{i}"):
            received(gather_z(i))
        start(gather_x(i))

    def unpack(i):
        h, ms = GROUPS[i]
        with scope(f"wait_gx{i}"):
            received(gather_x(i))
        for n, m in enumerate(ms):
            fresh = decode_root(nc[i, :, :, pl.ds(8 * n, 8), :].reshape(FEAT, FEAT), old[h, m])
            hi, lo = split(fresh)
            nb[m, 0] = hi
            nb[m, 1] = lo
            g[h, m] = fresh

    def gate(h):
        unpack(2 * h)

        @pl.loop(0, TOK // BLK, unroll=True)
        def _(i):
            begin = pl.multiple_of(i * BLK, BLK)
            qt = q[pl.ds(begin, BLK), cols(h)]
            p1 = mm(qt, nb[0, 0], NT) + mm(qt, nb[0, 1], NT)
            p3 = mm(qt, nb[1, 0], NT) + mm(qt, nb[1, 1], NT)
            hi, lo = split(p1 * sigmoid(p1) * p3)
            act[0, pl.ds(begin, BLK), :] = hi
            act[1, pl.ds(begin, BLK), :] = lo

    def project(h):
        unpack(2 * h + 1)

        @pl.loop(0, TOK // BLK, unroll=True)
        def _(i):
            part = pl.ds(pl.multiple_of(i * BLK, BLK), BLK)
            hi, lo = act[0, part, :], act[1, part, :]
            o = mm(hi, nb[2, 0], NT) + mm(lo, nb[2, 0], NT) + mm(hi, nb[2, 1], NT)
            z[part, cols(h)] = o * hscale[h]

    def send_if(which, *names):
        @pl.when(which)
        def _():
            send(*names)

    x_sum(0)
    x_sum(1)
    with scope("attn02"):
        attend(0, 2)
    x_sum(2)
    x_sum(3)
    with scope("attn03"):
        attend(0, 3)
    renorm(0)
    renorm(1)
    with scope("far"):

        @pl.when(s < last)
        def _():
            await_query()
            far_part()

    send("attn_leg")
    renorm(2)
    renorm(3)
    send("total")
    send_if(me_h % 2 == 0, "attn", "attn0")
    spread(0)
    spread(1)
    with scope("attn12"):
        attend(1, 2)
    with scope("wait_v"):

        @pl.when(s > 0)
        def _():
            v_copy().wait_recv()

    with scope("attn01"):
        attend(0, 1)
    spread(2)
    spread(3)
    send_if(me_h % 2 == 1, "attn", "attn0")
    with scope("attn13"):
        attend(1, 3)
    with scope("gate0"):
        gate(0)
    with scope("project0"):
        project(0)
    with scope("forward_o"):
        pass_on(attn_leg, "attn_forward")
    with scope("gate1"):
        gate(1)
    with scope("project1"):
        project(1)

    packed = jnp.zeros((128, 128), F32)
    for r in range(TOK // 128):
        zt = z[pl.ds(r * 128, 128), :]
        packed = jnp.where(lane == r, jnp.sum(zt * zt, axis=1, keepdims=True), packed)
    sq[0] = packed.T[:8, :]
    sqs = [
        remote(sq.at[0], sq.at[d], sq_s.at[d - 1], sq_r.at[d - 1], {"head": (me_h + d) % HS})
        for d in range(1, HS)
    ]
    start(sqs)

    for h in range(2):
        for m in range(3):
            nout[m, h] = g[h, m].T

    with scope("near"):
        near_part()

    with scope("wait_sq"):
        for copy in sqs:
            copy.wait_recv()
    total = sq[0]
    for d in range(1, HS):
        total = total + sq[d]
    inv = 1.0 / jnp.sqrt(total / (2 * HS * FEAT) + EPS)
    inv_out[...] = jnp.concatenate([inv, jnp.zeros((120, 128), F32)], axis=0).T
    with scope("wait_end"):
        for i in range(4):
            for copy in reduce_x(i) + reduce_z(i) + gather_z(i) + gather_x(i):
                copy.wait_send()
        for copy in sqs:
            copy.wait_send()
        drain_halo()


def combine(attn, z, inv, fresh, mixed_hbm, n1_hbm, n3_hbm, n2_hbm, out, sem):
    copies = [
        pltpu.make_async_copy(fresh.at[m], ref, sem.at[8 + m])
        for m, ref in enumerate((n1_hbm, n3_hbm, n2_hbm))
    ]
    for copy in copies:
        copy.start()
    scale = inv[...]
    for r in range(TOK // 128):
        part = pl.ds(r * 128, 128)
        out[part, :] = attn[part, :] + z[part, :] * scale[:, r : r + 1]
        copy = pltpu.make_async_copy(out.at[part, :], mixed_hbm.at[part, :], sem.at[r])
        copy.start()
        copies.append(copy)
    for copy in copies:
        copy.wait()


def per_device(queries, keys, values, rates, head_scale, w_one, w_three, w_two):
    any_space = pl.BlockSpec(memory_space=pltpu.HBM)
    vmem = pl.BlockSpec(memory_space=pltpu.VMEM)
    dma = pltpu.SemaphoreType.DMA
    rows = jax.ShapeDtypeStruct((TOK, 2 * FEAT), F32)
    weight = jax.ShapeDtypeStruct((2, FEAT, FEAT), F32)
    pinned = [
        pltpu.with_memory_space_constraint(a, pltpu.HBM) for a in (queries, keys, values, rates.T, head_scale, w_one, w_three, w_two)
    ]
    attn, z, inv, fresh = pl.pallas_call(
        layer,
        out_shape=(rows, rows, jax.ShapeDtypeStruct((128, 128), F32), jax.ShapeDtypeStruct((3, 2, FEAT, FEAT), F32)),
        in_specs=[any_space] * 8,
        out_specs=(vmem,) * 4,
        scratch_shapes=[
            pltpu.VMEM((TOK, 2 * FEAT), BF16),
            pltpu.VMEM((TOK, 2 * FEAT), BF16),
            pltpu.VMEM((TOK, 2 * FEAT), BF16),
            pltpu.VMEM((2, TOK), F32),
            pltpu.SMEM((2,), F32),
            pltpu.VMEM((3, 2, FEAT, FEAT), F32),
            pltpu.VMEM((2, 3, FEAT, FEAT), F32),
            pltpu.VMEM((2, 3, 2, FEAT, FEAT), BF16),
            pltpu.VMEM((2, 3, FEAT, 1), F32),
            pltpu.VMEM((6, FEAT, TOK), BF16),
            pltpu.VMEM((2, 3, FEAT, FEAT), F32),
            pltpu.VMEM((4, XS, 136, FEAT), BF16),
            pltpu.VMEM((4, XS - 1, 136, FEAT), BF16),
            pltpu.VMEM((2, 3, 64, FEAT), F32),
            pltpu.VMEM((4, ZS, 24, FEAT), BF16),
            pltpu.VMEM((4, ZS - 1, 24, FEAT), BF16),
            pltpu.VMEM((4, XS, ZS, 16, FEAT), BF16),
            pltpu.VMEM((3, 2, FEAT, FEAT), BF16),
            pltpu.VMEM((2, TOK, FEAT), BF16),
            pltpu.VMEM((HS, 8, 128), F32),
            pltpu.VMEM((BLK, FEAT), BF16),
            pltpu.VMEM((BLK, FEAT), BF16),
            pltpu.VMEM((BLK, FEAT), BF16),
            pltpu.VMEM((WINDOW, FEAT), BF16),
            pltpu.VMEM((BLK, FEAT), BF16),
            pltpu.VMEM((WINDOW, FEAT), BF16),
            pltpu.VMEM((16, 128), F32),
            pltpu.VMEM((16, 128), F32),
            pltpu.VMEM((16, 128), F32),
            pltpu.VMEM((16, 128), F32),
            pltpu.VMEM((2, BLK + 8, FEAT), BF16),
            pltpu.VMEM((BLK + 8, FEAT), BF16),
            pltpu.VMEM((2, BLK + 8, FEAT), BF16),
            pltpu.VMEM((BLK + 8, FEAT), BF16),
            pltpu.VMEM((2, BLK + 8, FEAT), BF16),
            dma((14,)),
            dma((14,)),
            dma((11,)),
            dma((4, XS - 1)),
            dma((4, XS - 1)),
            dma((4, ZS - 1)),
            dma((4, ZS - 1)),
            dma((4, ZS - 1)),
            dma((4, ZS - 1)),
            dma((4, XS - 1)),
            dma((4, XS - 1)),
            dma((HS - 1,)),
            dma((HS - 1,)),
        ],
        compiler_params=pltpu.CompilerParams(
            collective_id=0, has_side_effects=True, vmem_limit_bytes=44 * 1024 * 1024
        ),
        name="layer",
    )(*pinned)
    return pl.pallas_call(
        combine,
        out_shape=(rows, weight, weight, weight),
        in_specs=[vmem] * 4,
        out_specs=(any_space,) * 4,
        scratch_shapes=[pltpu.VMEM((TOK, 2 * FEAT), F32), dma((11,))],
        compiler_params=pltpu.CompilerParams(vmem_limit_bytes=16 * 1024 * 1024),
        name="combine",
    )(attn, z, inv, fresh)


def solution(mesh):
    tile = P("seq", "head")
    weight = P("head", None, None)
    return jax.shard_map(
        per_device,
        mesh=mesh,
        in_specs=(tile, tile, tile, tile, P("head"), weight, weight, weight),
        out_specs=(tile, weight, weight, weight),
        check_vma=False,
    )
```

time: 61 us -> 58.1 us (0.952)
  Pallas kernels: 60.3 us -> 57.2 us
    pallas_call x1, Pallas kernels: 58.4 us -> 55.3 us  [per_device(): pl.pallas_call(layer, out_shape=(rows, rows, jax.ShapeDtypeStruct((128, 1...]
where the time goes in v3:
time: 58.1 us; the launch traced here: 58 us
  Pallas kernels  57.2 us (98%)
  between operations  0.8 us (1%)
    pallas_call x1, Pallas kernels, per_device(): pl.pallas_call(layer, out_shape=(rows, rows, jax.ShapeDtypeStruct((128, 1...  55.3 us
    pallas_call x1, Pallas kernels, per_device(): pl.pallas_call(combine, out_shape=(rows, weight, weight, weight), in_spec...  1.92 us

profile of v3, /device:TPU:1, one launch (start us, length us, event | category | flops | bytes accessed | tf_op | source)
XLA Modules:
  0.0 58.0 jit_solution(12436942142549610532)
XLA Ops:
  0.6 55.3 %layer.1 = (f32[1024,512]{1,0:T(8,128)S(1)}, f32[1024,512]{1,0:T(8,128)S(1)}, f32[128,128]{1,0:T(8,128)S(1)}, f32[3,2,256,256]{3,2,1,0:T(8,128)S(1)}) custom-call(bf16[1024,512]{1,0:T(8,128)(2,1)} %q_hbm.1, bf16[1024,512]{1,0:T(8,128)(2,1)} %k_hbm.1, bf16[1024,512]{1,0:T(8,128)(2,1)} %v_hbm.1, f32[2,1024]{1,0:T(2,128)} %bitcast.1, f32[2]{0:T(128)} %hscale_hbm.1, ...), custom_call_target="tpu_custom_call" | custom-call | tf_op jit(solution)/shard_map/layer/pallas_call | solution.py:702
  55.9 1.9 %combine.1 = (f32[1024,512]{1,0:T(8,128)}, f32[2,256,256]{2,1,0:T(8,128)}, f32[2,256,256]{2,1,0:T(8,128)}, f32[2,256,256]{2,1,0:T(8,128)}) custom-call(f32[1024,512]{1,0:T(8,128)S(1)} %get-tuple-element.8.attn, f32[1024,512]{1,0:T(8,128)S(1)} %get-tuple-element.9.z, f32[128,128]{1,0:T(8,128)S(1)} %get-tuple-element.10.inv, ...), custom_call_target="tpu_custom_call" | custom-call | tf_op jit(solution)/shard_map/combine/pallas_call | solution.py:762
